TPU v7x, 128 devices: a whole 4x4x4 slice. The times are simulated.
128 devices in a mesh: prow: 8 (over y, x_lo), pcol: 16 (over x_hi, z, core).
Axes of the slice: x: 4 (x_hi: 2, x_lo: 2; x = x_hi * 2 + x_lo), y: 4, z: 4, core: 2. Of those that a mesh axis runs over, the one named last changes fastest.
Arguments:
- covariance: float32 [16384, 16384], P(('prow', 'pcol')), may hold values from -600 to 600, as said below
- factor_left: float32 [64, 16384], P(None, ('prow', 'pcol')), may hold values from -6 to 6
- factor_right: float32 [64, 16384], P('prow', 'pcol'), may hold values from -3 to 3
Outputs:
- whitened: float32 [16384, 16384], P('prow', 'pcol')
Inputs may be any that keep to these rules, and one draw needn't show every extreme that they name: `covariance`: entries are real-valued and of full rank.
All inputs are finite; a program needn't handle non-finite values.
Results may differ from a plain program's by a relative error of at most 0.00007.
Values sent between devices are 32-bit elements; how exact they have to be, the bound alone decides.
No kernel may reach another device: no remote copies, remote signals or barrier semaphores. Data moves between devices by JAX's collectives and lax.ppermute only.
A program may use at most 128 MiB of HBM per device.

v0:
```python
import jax
import jax.numpy as jnp
from jax import lax
from jax.sharding import PartitionSpec as P

ORDER = 16384
TILE = 64


epsilon = 1e-06


def in_order(blocks, dim):
    blocks = jnp.moveaxis(blocks, 0, dim)
    shape = blocks.shape
    return blocks.reshape(*shape[:dim], shape[dim] * shape[dim + 1], *shape[dim + 2 :])


def copy_for_each(shard, axis):
    length = lax.axis_size(axis)
    return lax.all_to_all(
        jnp.broadcast_to(shard[None], (length, *shard.shape)), axis, 0, 0, tiled=True
    )


def collect(shard, axis, dim):
    return in_order(copy_for_each(shard, axis), dim)


def over_copies(shard, axis):
    everything = copy_for_each(shard, axis)
    return jnp.sum(everything, axis=0)


def deal_columns(source):
    height = source.shape[0]
    breadth = source.shape[1]
    grid_cols = lax.axis_size("pcol")
    arranged = (
        source.reshape(height, breadth // (TILE * grid_cols), grid_cols, TILE)
        .transpose(0, 2, 1, 3)
        .reshape(height, breadth)
    )
    return lax.all_to_all(arranged, "pcol", split_axis=1, concat_axis=0, tiled=True)


def order_rows(source):
    height = source.shape[0]
    breadth = source.shape[1]
    grid_rows = lax.axis_size("prow")
    grouped = source.reshape(height // (TILE * grid_rows), grid_rows, TILE, breadth)
    return grouped.transpose(1, 0, 2, 3).reshape(height, breadth)


def body(covariance, factor_left, factor_right):
    right_panel = collect(factor_right, "prow", 0)
    dealt = deal_columns(covariance)
    left_block = collect(factor_left, "pcol", 1).T
    tiles_moved, left_rows = (
        lax.all_to_all(order_rows(dealt), "prow", split_axis=0, concat_axis=0, tiled=True),
        lax.all_to_all(order_rows(left_block), "prow", split_axis=0, concat_axis=0, tiled=True),
    )
    corrected = tiles_moved + jnp.dot(
        left_rows, right_panel, precision=lax.Precision.HIGHEST, preferred_element_type=jnp.float32
    )
    squared = corrected * corrected
    row_total = over_copies(jnp.sum(squared, axis=1), "pcol")
    col_total = over_copies(jnp.sum(squared, axis=0), "prow")
    row_mean = row_total / ORDER + epsilon
    col_mean = col_total / ORDER + epsilon
    return corrected * lax.rsqrt(jnp.sqrt(row_mean[:, None] * col_mean[None, :]))


def solution(mesh):
    placed = (P(("prow", "pcol"), None), P(None, ("prow", "pcol")), P("prow", "pcol"))
    return jax.shard_map(
        body, mesh=mesh, in_specs=placed, out_specs=P("prow", "pcol"), check_vma=False
    )
```

profile of v0, /device:TPU:1, one launch (start us, length us, event | category | flops | bytes accessed | tf_op | source)
XLA Modules:
  0.0 340.6 jit_solution(234733590115165641)
XLA Ops:
  0.0 0.8 broadcast_in_dim.9
  0.8 11.9 %all_to_all.62 = f32[8,8,1024]{2,1,0:T(8,128)S(1)} all-to-all(f32[8,8,1024]{2,1,0:T(8,128)S(1)} %broadcast_in_dim.9), channel_id=1, replica_groups=mesh['prow'=8,'pcol'=16] {'prow'}, dimensions={0} | all-to-all | bytes 524288 | tf_op jit(solution)/shard_map/all_to_all | solution.py:21
  12.7 1.7 broadcast_in_dim.8
  14.3 9.6 %all-to-all-start.2 = ((f32[16,64,128]{2,1,0:T(8,128)}), f32[16,64,128]{2,1,0:T(8,128)S(1)}, u32[]{:S(2)}, u32[]{:S(2)}) async-start(f32[16,64,128]{2,1,0:T(8,128)} %broadcast_in_dim.8), calls=%async_computation.2 | async-start | bytes 1048576 | tf_op jit(solution)/shard_map/all_to_all | solution.py:21
  23.9 9.0 %copy.28 = f32[128,16384]{0,1:T(8,128)} copy(f32[128,16384]{1,0:T(8,128)} %param.3) | data formatting | bytes 16777216 | tf_op args[0]
  32.9 8.3 %copy.29 = f32[128,16,16,64]{0,3,2,1:T(8,128)} copy(f32[128,16,16,64]{0,3,1,2:T(8,128)} %bitcast.37) | data formatting | bytes 16777216 | tf_op jit(solution)/shard_map/transpose | solution.py:41
  41.1 0.0 all-to-all-done.2
  41.1 7.2 %all-to-all-start = ((f32[128,16,1024]{0,2,1:T(8,128)}), f32[128,16,1024]{0,2,1:T(8,128)}, u32[]{:S(2)}, u32[]{:S(2)}) async-start(f32[128,16,1024]{0,2,1:T(8,128)} %bitcast.34), calls=%async_computation | async-start | bytes 16777216 | tf_op jit(solution)/shard_map/all_to_all | solution.py:44
  48.4 0.4 reshape.54
  48.8 0.3 copy.43
  49.1 1.4 all_to_all.49
  50.5 117.8 %all-to-all-done = f32[128,16,1024]{0,2,1:T(8,128)} async-done(((f32[128,16,1024]{0,2,1:T(8,128)}), f32[128,16,1024]{0,2,1:T(8,128)}, u32[]{:S(2)}, u32[]{:S(2)}) %all-to-all-start) | async-done | bytes 8388640 | tf_op jit(solution)/shard_map/all_to_all | solution.py:44
  168.4 3.5 %all-to-all-start.3 = ((f32[8,256,64]{1,2,0:T(8,128)}), f32[8,256,64]{1,2,0:T(8,128)S(1)}, u32[]{:S(2)}, u32[]{:S(2)}) async-start(f32[8,256,64]{1,2,0:T(8,128)} %all_to_all.49), calls=%async_computation.3 | async-start | bytes 1048576 | tf_op jit(solution)/shard_map/all_to_all | solution.py:61
  171.9 9.2 %copy.30 = f32[16,128,1024]{2,1,0:T(8,128)} copy(f32[16,128,1024]{1,2,0:T(8,128)} %bitcast.3) | data formatting | bytes 16777216 | tf_op jit(solution)/shard_map/all_to_all | solution.py:44
  181.1 8.3 %copy.31 = f32[8,4,64,1024]{3,2,1,0:T(8,128)} copy(f32[8,4,64,1024]{3,2,0,1:T(8,128)} %bitcast.36) | data formatting | bytes 16777216 | tf_op jit(solution)/shard_map/transpose | solution.py:52
  189.4 0.0 all-to-all-done.3
  189.4 5.1 %all-to-all-start.1 = ((f32[8,256,1024]{2,1,0:T(8,128)}), f32[8,256,1024]{2,1,0:T(8,128)}, u32[]{:S(2)}, u32[]{:S(2)}) async-start(f32[8,256,1024]{2,1,0:T(8,128)} %bitcast.35), calls=%async_computation.1 | async-start | bytes 16777216 | tf_op jit(solution)/shard_map/all_to_all | solution.py:60
  194.5 93.2 %all-to-all-done.1 = f32[8,256,1024]{2,1,0:T(8,128)} async-done(((f32[8,256,1024]{2,1,0:T(8,128)}), f32[8,256,1024]{2,1,0:T(8,128)}, u32[]{:S(2)}, u32[]{:S(2)}) %all-to-all-start.1) | async-done | bytes 8388640 | tf_op jit(solution)/shard_map/all_to_all | solution.py:60
  287.7 12.0 %multiply_reduce_fusion.1 = (f32[2048]{0:T(1024)S(1)}, f32[1024]{0:T(1024)S(1)}, f32[2048,1024]{1,0:T(8,128)}) fusion(f32[2048,64]{0,1:T(8,128)S(1)} %bitcast.39, f32[8,8,1024]{2,1,0:T(8,128)S(1)} %all_to_all.62, f32[8,256,1024]{2,1,0:T(8,128)} %all-to-all-done.1), kind=kOutput, calls=%fused_computation.3 | convolution fusion | flops 1618998272 | bytes 17575936 | tf_op jit(solution)/shard_map/dot_general | solution.py:63
  299.8 9.0 %all_to_all.63 = f32[8,1,1024]{2,1,0:T(1,128)S(1)} all-to-all(f32[8,1,1024]{2,1,0:T(1,128)S(1)} %broadcast_in_dim.11), channel_id=1, replica_groups=mesh['prow'=8,'pcol'=16] {'prow'}, dimensions={0} | all-to-all | bytes 65536 | tf_op jit(solution)/shard_map/all_to_all | solution.py:21
  308.8 0.7 broadcast_in_dim.10
  309.5 16.3 %all-to-all-start.5 = ((f32[16,1,2048]{2,1,0:T(1,128)}), f32[16,1,2048]{2,1,0:T(1,128)S(1)}, u32[]{:S(2)}, u32[]{:S(2)}) async-start(f32[16,1,2048]{2,1,0:T(1,128)} %broadcast_in_dim.10), calls=%async_computation.5 | async-start | bytes 262144 | tf_op jit(solution)/shard_map/all_to_all | solution.py:21
  325.8 7.6 %all-to-all-done.5 = f32[16,1,2048]{2,1,0:T(1,128)S(1)} async-done(((f32[16,1,2048]{2,1,0:T(1,128)}), f32[16,1,2048]{2,1,0:T(1,128)S(1)}, u32[]{:S(2)}, u32[]{:S(2)}) %all-to-all-start.5) | async-done | bytes 131104 | tf_op jit(solution)/shard_map/all_to_all | solution.py:21
  333.4 0.1 reduce_sum.37
  333.5 7.1 %rsqrt_multiply_fusion = f32[2048,1024]{1,0:T(8,128)} fusion(f32[2048,1024]{1,0:T(8,128)} %get-tuple-element.7, f32[1024]{0:T(1024)S(1)} %multiply_add_fusion.1, f32[2048]{0:T(1024)S(1)} %multiply_add_fusion), kind=kLoop, calls=%fused_computation.1 | loop fusion | flops 4194304 | bytes 16789504 | tf_op jit(solution)/shard_map/mul | solution.py:71
  (6 shorter events, 0.1 us)
Async XLA Ops:
  14.3 26.8 %all-to-all-start.2 = ((f32[16,64,128]{2,1,0:T(8,128)}), f32[16,64,128]{2,1,0:T(8,128)S(1)}, u32[]{:S(2)}, u32[]{:S(2)}) async-start(f32[16,64,128]{2,1,0:T(8,128)} %broadcast_in_dim.8), calls=%async_computation.2 | async-start | bytes 1048576 | tf_op jit(solution)/shard_map/all_to_all | solution.py:21
  41.1 127.2 %all-to-all-start = ((f32[128,16,1024]{0,2,1:T(8,128)}), f32[128,16,1024]{0,2,1:T(8,128)}, u32[]{:S(2)}, u32[]{:S(2)}) async-start(f32[128,16,1024]{0,2,1:T(8,128)} %bitcast.34), calls=%async_computation | async-start | bytes 16777216 | tf_op jit(solution)/shard_map/all_to_all | solution.py:44
  168.4 21.0 %all-to-all-start.3 = ((f32[8,256,64]{1,2,0:T(8,128)}), f32[8,256,64]{1,2,0:T(8,128)S(1)}, u32[]{:S(2)}, u32[]{:S(2)}) async-start(f32[8,256,64]{1,2,0:T(8,128)} %all_to_all.49), calls=%async_computation.3 | async-start | bytes 1048576 | tf_op jit(solution)/shard_map/all_to_all | solution.py:61
  189.4 98.3 %all-to-all-start.1 = ((f32[8,256,1024]{2,1,0:T(8,128)}), f32[8,256,1024]{2,1,0:T(8,128)}, u32[]{:S(2)}, u32[]{:S(2)}) async-start(f32[8,256,1024]{2,1,0:T(8,128)} %bitcast.35), calls=%async_computation.1 | async-start | bytes 16777216 | tf_op jit(solution)/shard_map/all_to_all | solution.py:60
  309.5 23.9 %all-to-all-start.5 = ((f32[16,1,2048]{2,1,0:T(1,128)}), f32[16,1,2048]{2,1,0:T(1,128)S(1)}, u32[]{:S(2)}, u32[]{:S(2)}) async-start(f32[16,1,2048]{2,1,0:T(1,128)} %broadcast_in_dim.10), calls=%async_computation.5 | async-start | bytes 262144 | tf_op jit(solution)/shard_map/all_to_all | solution.py:21
where the time goes:
time: 342 us; the launch traced here: 341 us
  waiting for transfers between devices  219 us (64%)
  starting transfers between devices  41.6 us (12%)
  local copies, waits for them, and re-layouts  40.1 us (12%)
  blocking collectives  20.9 us (6%)
  matrix products  12 us (4%)
  other arithmetic  7.22 us (2%)
    all_to_all x1, waiting for transfers between devices, deal_columns(): lax.all_to_all(arranged, 'pcol', split_axis=1, concat_axis=0, tiled=True)  118 us
    all_to_all x1, waiting for transfers between devices, body(): lax.all_to_all(order_rows(dealt), 'prow', split_axis=0, concat_axis=0, ti...  93.2 us
    all_to_all x2, starting transfers between devices, copy_for_each(): lax.all_to_all(jnp.broadcast_to(shard[None], (length, *shard.shape)), axi...  25.9 us
    all_to_all x2, blocking collectives, copy_for_each(): lax.all_to_all(jnp.broadcast_to(shard[None], (length, *shard.shape)), axi...  20.9 us
    dot_general x1, matrix products, body(): jnp.dot(left_rows, right_panel, precision=lax.Precision.HIGHEST, preferre...  12 us
    all_to_all x1, local copies, waits for them, and re-layouts, deal_columns(): lax.all_to_all(arranged, 'pcol', split_axis=1, concat_axis=0, tiled=True)  9.25 us
    unnamed x1, local copies, waits for them, and re-layouts  8.98 us
    transpose x1, local copies, waits for them, and re-layouts, deal_columns(): arranged = source.reshape(height, breadth // (TILE * grid_cols), grid_col...  8.26 us
  transfers between devices with their start and end apart: 5, of which 3 were waited for; matrix products, arithmetic and copies ran while one was open for 10% of the time, Pallas kernels for 0%

commit v1 on v0

v1 whole, which is shorter than its diff:
```python
import functools

import jax
import jax.numpy as jnp
from jax import lax
from jax.experimental import pallas as pl
from jax.experimental.pallas import tpu as pltpu
from jax.sharding import Mesh
from jax.sharding import PartitionSpec as P


ORDER = 16384
TILE = 64
epsilon = 1e-06
F32 = jnp.float32

NAMES = ("y", "xl", "xh", "z1", "z0", "c")
ROWS = ("y", "xl")
COLS = ("xh", "z1", "z0", "c")
ZC = ("z1", "z0", "c")
SPREAD = ("y", "xl", "xh", "z1")

CHUNKS = (1, 3)


def flip(pairing, dz, dc):
    pairs = []
    for z1 in range(2):
        for z0 in range(2):
            for c in range(2):
                to = z1 ^ (dz if pairing == 2 else 0), z0 ^ dz, c ^ dc
                pairs.append((z1 * 4 + z0 * 2 + c, to[0] * 4 + to[1] * 2 + to[2]))
    return pairs


def pack_kernel(with_left, x_ref, *refs):
    if with_left:
        left_ref, refs = refs[0], refs[1:]
    z0 = lax.axis_index("z0")
    odd = lax.axis_index("c") == 1
    r = pl.program_id(0)
    low = lax.broadcasted_iota(jnp.int32, (TILE, 128), 1) < TILE
    for dz in range(2):
        for xh in range(2):
            for z1 in range(2):
                at = pl.multiple_of((xh * 4 + z1 * 2 + (z0 ^ dz)) * 128, 128)
                a = x_ref[:, pl.ds(at, 128)]
                b = x_ref[:, pl.ds(at + 1024, 128)]
                even_tiles = jnp.where(low, a, pltpu.roll(b, 64, 1))
                odd_tiles = jnp.where(low, pltpu.roll(a, 64, 1), b)
                slot = xh * 2 + z1
                refs[dz * 2][slot, 0:TILE, :] = jnp.where(odd, odd_tiles, even_tiles)
                refs[dz * 2 + 1][slot, 0:TILE, :] = jnp.where(odd, even_tiles, odd_tiles)
    if with_left:
        both = left_ref[...]
        shifted = pltpu.roll(both, 64, 1)
        top = jnp.where(r == 0, both, shifted)
        bottom = jnp.where(r == 0, shifted, both)
        packed = jnp.where(low[0:32], top[0:32], bottom[32:64])
        for ref in refs:
            for slot in range(4):
                ref[slot, TILE : TILE + 32, :] = packed


def pack(x, left, start, count):
    with_left = left is not None
    height = TILE + 32 if with_left else TILE
    assert count == 1 or not with_left
    in_specs = [pl.BlockSpec((TILE, 2048), lambda r, j: (r, start + j))]
    args = [x]
    if with_left:
        in_specs.append(pl.BlockSpec((64, 128), lambda r, j: (0, 0)))
        args.append(left)
    return pl.pallas_call(
        functools.partial(pack_kernel, with_left),
        grid=(2, count),
        in_specs=in_specs,
        out_specs=[pl.BlockSpec((4, height, 128), lambda r, j: (r, j, 0))] * 4,
        out_shape=[jax.ShapeDtypeStruct((8, height * count, 128), F32)] * 4,
        name="pack",
    )(*args)


def assemble_kernel(heights, *refs):
    pieces, out_ref = refs[:-1], refs[-1]
    own = lax.axis_index("z0") * 2 + lax.axis_index("c")
    at = 0
    for g, height in enumerate(heights):
        for d in range(4):
            out_ref[own ^ d, :, at : at + height, :] = pieces[g * 4 + d][...]
        at += height


def assemble(groups):
    heights = tuple(g[0].shape[1] for g in groups)
    total = sum(heights)
    whole = pl.pallas_call(
        functools.partial(assemble_kernel, heights),
        grid=(8,),
        in_specs=[pl.BlockSpec((1, h, 128), lambda i: (i, 0, 0)) for h in heights for _ in range(4)],
        out_specs=pl.BlockSpec((4, 1, total, 128), lambda i: (0, i, 0, 0)),
        out_shape=jax.ShapeDtypeStruct((4, 8, total, 128), F32),
        name="assemble",
    )(*[p for g in groups for p in g])
    return whole.reshape(32, total, 128)


def correct_kernel(offsets, swapped, got_ref, left_ref, right_ref, out_ref, row_ref, col_ref):
    step = pl.program_id(0)
    product = jnp.dot(left_ref[...], right_ref[...], preferred_element_type=F32)
    turn = (lax.axis_index("y") // 2) ^ lax.axis_index("z0")
    row_acc = jnp.zeros((256, 128), F32)

    @pl.when(step == 0)
    def _():
        col_ref[...] = jnp.zeros_like(col_ref)

    for j, (at, swap) in enumerate(zip(offsets, swapped)):
        cols = slice(j * 128, j * 128 + 128)
        parts = []
        for k in range(4):
            source = (k ^ turn) if swap else k
            parts.append(got_ref[source, at : at + TILE, :] + product[k * TILE : k * TILE + TILE, cols])
        tile = jnp.concatenate(parts, 0)
        out_ref[:, cols] = tile
        square = tile * tile
        row_acc = row_acc + square
        col_ref[:, cols] += jnp.sum(square.reshape(32, 8, 128), 0)
    row_ref[0] = lax.dot_general(
        jnp.ones((8, 128), F32),
        row_acc,
        (((1,), (1,)), ((), ())),
        precision=lax.Precision.HIGHEST,
        preferred_element_type=F32,
    )


def correct(got, left, right, start, offsets, swapped):
    width = 128 * len(offsets)
    assert (start * 128) % width == 0
    return pl.pallas_call(
        functools.partial(correct_kernel, offsets, swapped),
        grid=(8,),
        in_specs=[
            pl.BlockSpec((4, got.shape[1], 128), lambda i: (i, 0, 0)),
            pl.BlockSpec((256, 256), lambda i: (i, 0)),
            pl.BlockSpec((256, width), lambda i: (0, 0)),
        ],
        out_specs=[
            pl.BlockSpec((256, width), lambda i: (i, 0)),
            pl.BlockSpec((1, 8, 256), lambda i: (i, 0, 0)),
            pl.BlockSpec((8, width), lambda i: (0, 0)),
        ],
        out_shape=[
            jax.ShapeDtypeStruct((2048, width), F32),
            jax.ShapeDtypeStruct((8, 8, 256), F32),
            jax.ShapeDtypeStruct((8, width), F32),
        ],
        name="correct",
    )(got, left, right)


def scale_kernel(widths, *refs):
    n = len(widths)
    row_ref, col_ref, out_ref = refs[n:]
    row = jnp.transpose(jnp.broadcast_to(row_ref[0], (128, 256)))
    at = 0
    for ref, width in zip(refs, widths):
        for j in range(width // 128):
            cols = slice(at, at + 128)
            out_ref[:, cols] = ref[:, j * 128 : j * 128 + 128] * (row * col_ref[:, cols])
            at += 128


def scale(parts, row, col):
    widths = tuple(p.shape[1] for p in parts)
    return pl.pallas_call(
        functools.partial(scale_kernel, widths),
        grid=(8,),
        in_specs=[pl.BlockSpec((256, w), lambda i: (i, 0)) for w in widths]
        + [pl.BlockSpec((1, 1, 256), lambda i: (i, 0, 0)), pl.BlockSpec((1, 1024), lambda i: (0, 0))],
        out_specs=pl.BlockSpec((256, 1024), lambda i: (i, 0)),
        out_shape=jax.ShapeDtypeStruct((2048, 1024), F32),
        name="scale",
    )(*parts, row.reshape(8, 1, 256), col.reshape(1, 1024))


def split(x):
    high = lax.reduce_precision(x, 8, 7)
    low = lax.reduce_precision(x - high, 8, 7)
    return high.astype(jnp.bfloat16), low.astype(jnp.bfloat16)


ROUNDS = (
    ("xl", [(0, 1), (1, 0)], lambda: lax.axis_index("xl")),
    ("y", [(0, 1), (1, 0), (2, 3), (3, 2)], lambda: lax.axis_index("y") % 2),
    ("y", [(0, 2), (2, 0), (1, 3), (3, 1)], lambda: lax.axis_index("y") // 2),
)


def gather_right(part):
    for axis, pairs, bit in ROUNDS:
        other = lax.ppermute(part, axis, pairs)
        first = bit() == 0
        part = jnp.where(first, jnp.concatenate([part, other]), jnp.concatenate([other, part]))
    return part


def sum_over_rows_of_grid(part):
    for axis, pairs, _ in ROUNDS:
        part = part + lax.ppermute(part, axis, pairs)
    return part


def sum_over_cols_of_grid(part):
    length = lax.axis_size(COLS)
    copies = jnp.broadcast_to(part[None], (length, *part.shape))
    return jnp.sum(lax.all_to_all(copies, COLS, 0, 0, tiled=True), axis=0)


def trade(pieces, pairing):
    out = [pieces[0]]
    for d in (1, 2, 3):
        out.append(lax.ppermute(pieces[d], ZC, flip(pairing, d // 2, d % 2)))
    return out


def body(covariance, factor_left, factor_right):
    start = 0
    traded = []
    for n in CHUNKS:
        groups = []
        for pairing in (1, 2):
            pieces = pack(covariance, factor_left if start == 0 else None, start, n)
            groups.append(trade(pieces, pairing))
            start += n
        traded.append(groups)

    got = []
    for groups in traded:
        whole = assemble(groups)
        got.append(lax.all_to_all(whole, SPREAD, 0, 0, tiled=True))

    panel = gather_right(factor_right)
    high, low = split(panel)
    right = jnp.concatenate([high, low, high, low])
    packed = got[0][:, TILE : TILE + 32, :].reshape(32, 32, 2, TILE)
    left = packed.transpose(0, 3, 2, 1).reshape(2048, 64)
    high, low = split(left)
    left = jnp.concatenate([high, high, low, low], axis=1)

    parts, row_parts, col_parts = [], [], []
    start = 0
    for i, n in enumerate(CHUNKS):
        first = TILE + 32 if i == 0 else TILE * n
        offsets = tuple(j * TILE for j in range(n)) + tuple(first + j * TILE for j in range(n))
        swapped = (False,) * n + (True,) * n
        part, row, col = correct(got[i], left, right[:, start * 128 : (start + 2 * n) * 128], 0, offsets, swapped)
        parts.append(part)
        row_parts.append(row[:, 0, :].reshape(16, 128))
        col_parts.append(jnp.sum(col, axis=0))
        start += 2 * n
    col_total = sum_over_rows_of_grid(jnp.concatenate(col_parts).reshape(8, 128)).reshape(1024)
    row_total = sum_over_cols_of_grid(sum(row_parts)).reshape(2048)
    row_factor = lax.rsqrt(jnp.sqrt(row_total / ORDER + epsilon))
    col_factor = lax.rsqrt(jnp.sqrt(col_total / ORDER + epsilon))
    return scale(parts, row_factor, col_factor)


def solution(mesh):
    fine = Mesh(mesh.devices.reshape(4, 2, 2, 2, 2, 2), NAMES)
    placed = (P(NAMES, None), P(None, NAMES), P(ROWS, COLS))
    return jax.shard_map(body, mesh=fine, in_specs=placed, out_specs=P(ROWS, COLS), check_vma=False)
```

time: 342 us -> 296 us (0.87)
  waiting for transfers between devices: 219 us -> 162 us
  Pallas kernels: 0 us -> 55.7 us
  local copies, waits for them, and re-layouts: 40.1 us -> 3.69 us
  starting transfers between devices: 41.6 us -> 65 us
  blocking collectives: 20.9 us -> 0 us
  matrix products: 12 us -> 0 us
    all_to_all x5 -> x3, waiting for transfers between devices: 219 us -> 7 us  [the longest x1 6.99 us: sum_over_cols_of_grid(): return jnp.sum(lax.all_to_all(copies, COLS, 0, 0, tiled=True), axis=0)]
    ppermute x0 -> x18, waiting for transfers between devices: none -> 155 us  [the longest x3 89 us: gather_right(): other = lax.ppermute(part, axis, pairs)]
    pallas_call x0 -> x9, Pallas kernels: none -> 55.7 us  [the longest x2 16.6 us: correct(): pl.pallas_call(functools.partial(correct_kernel, offsets, swapped), grid=...]
    all_to_all x2 -> x0, blocking collectives: 20.9 us -> none  [copy_for_each(): lax.all_to_all(jnp.broadcast_to(shard[None], (length, *shard.shape)), axi...]
    ppermute x0 -> x18, starting transfers between devices: none -> 20 us  [the longest x12 13 us: trade(): out.append(lax.ppermute(pieces[d], ZC, flip(pairing, d // 2, d % 2)))]
    transpose x3 -> x0, local copies, waits for them, and re-layouts: 16.6 us -> none  [the longest x1 8.26 us: deal_columns(): arranged = source.reshape(height, breadth // (TILE * grid_cols), grid_col...]
    dot_general x1 -> x0, matrix products: 12 us -> none  [body(): jnp.dot(left_rows, right_panel, precision=lax.Precision.HIGHEST, preferre...]
    all_to_all x3 -> x0, local copies, waits for them, and re-layouts: 10.7 us -> none  [the longest x1 9.25 us: deal_columns(): lax.all_to_all(arranged, 'pcol', split_axis=1, concat_axis=0, tiled=True)]
  transfers between devices with their start and end apart: 5 -> 21, of which waited for: 3 -> 12; matrix products, arithmetic and copies ran while one was open for 10% -> 3% of each run, Pallas kernels for 0% -> 10%
where the time goes in v1:
time: 296 us; the launch traced here: 294 us
  waiting for transfers between devices  162 us (55%)
  starting transfers between devices  65 us (22%)
  Pallas kernels  55.7 us (19%)
  other arithmetic  6.99 us (2%)
  local copies, waits for them, and re-layouts  3.69 us (1%)
    ppermute x3, waiting for transfers between devices, gather_right(): other = lax.ppermute(part, axis, pairs)  89 us
    ppermute x12, waiting for transfers between devices, trade(): out.append(lax.ppermute(pieces[d], ZC, flip(pairing, d // 2, d % 2)))  64.3 us
    all_to_all x1, starting transfers between devices, sum_over_cols_of_grid(): return jnp.sum(lax.all_to_all(copies, COLS, 0, 0, tiled=True), axis=0)  28.6 us
    pallas_call x2, Pallas kernels, correct(): pl.pallas_call(functools.partial(correct_kernel, offsets, swapped), grid=...  16.6 us
    all_to_all x2, starting transfers between devices, body(): got.append(lax.all_to_all(whole, SPREAD, 0, 0, tiled=True))  16.4 us
    pallas_call x4, Pallas kernels, pack(): pl.pallas_call(functools.partial(pack_kernel, with_left), grid=(2, count)...  16.3 us
    pallas_call x2, Pallas kernels, assemble(): pl.pallas_call(functools.partial(assemble_kernel, heights), grid=(8,), in...  13.5 us
    ppermute x12, starting transfers between devices, trade(): out.append(lax.ppermute(pieces[d], ZC, flip(pairing, d // 2, d % 2)))  13 us
  transfers between devices with their start and end apart: 21, of which 12 were waited for; matrix products, arithmetic and copies ran while one was open for 3% of the time, Pallas kernels for 10%

profile of v1, /device:TPU:1, one launch (start us, length us, event | category | flops | bytes accessed | tf_op | source)
XLA Modules:
  0.0 294.0 jit_solution(5505286593983859158)
XLA Ops:
  0.0 2.2 pack.5
  2.2 1.5 collective-permute-start.3
  3.7 2.4 pack.4
  6.1 0.1 collective-permute-start
  6.1 1.7 collective-permute-start.1
  7.9 0.3 collective-permute-start.2
  8.2 3.9 %collective-permute-start.4 = (f32[8,64,128]{2,1,0:T(8,128)S(1)}, f32[8,64,128]{2,1,0:T(8,128)S(1)}, u32[]{:S(2)}, u32[]{:S(2)}) collective-permute-start(f32[8,64,128]{2,1,0:T(8,128)S(1)} %copy-done.10), channel_id=1, source_target_pairs={{0,6},{1,7},{2,4},{3,5},{4,2},{5,3},{6,0},{7,1},{8,14},{9,15},{10,... | collective-permute-start | bytes 786440 | tf_op jit(solution)/shard_map/ppermute | solution.py:224
  12.1 0.0 collective-permute-done.3.refs_5_
  12.1 0.1 collective-permute-start.5
  12.2 6.7 %collective-permute-done.4.refs_6_ = f32[8,64,128]{2,1,0:T(8,128)S(1)} collective-permute-done((f32[8,64,128]{2,1,0:T(8,128)S(1)}, f32[8,64,128]{2,1,0:T(8,128)S(1)}, u32[]{:S(2)}, u32[]{:S(2)}) %collective-permute-start.4) | collective-permute-done | bytes 262176 | tf_op jit(solution)/shard_map/ppermute | solution.py:224
  18.9 5.6 %collective-permute-done.5.refs_7_ = f32[8,64,128]{2,1,0:T(8,128)S(1)} collective-permute-done((f32[8,64,128]{2,1,0:T(8,128)S(1)}, f32[8,64,128]{2,1,0:T(8,128)S(1)}, u32[]{:S(2)}, u32[]{:S(2)}) %collective-permute-start.5) | collective-permute-done | bytes 262176 | tf_op jit(solution)/shard_map/ppermute | solution.py:224
  24.5 0.0 collective-permute-done.refs_1_
  24.5 0.0 collective-permute-done.1.refs_2_
  24.5 1.4 collective-permute-done.2.refs_3_
  25.9 0.7 copy-done.4
  26.6 5.7 %assemble.2 = f32[4,8,160,128]{3,2,1,0:T(8,128)} custom-call(f32[8,96,128]{2,1,0:T(8,128)} %get-tuple-element.27.refs_0_, f32[8,96,128]{2,1,0:T(8,128)} %copy-done.2, f32[8,96,128]{2,1,0:T(8,128)} %copy-done.3, f32[8,96,128]{2,1,0:T(8,128)} %copy-done.4, f32[8,64,128]{2,1,0:T(8,128)} %get-tuple-element.31.refs_4_, f32[8,64,128]{2,1,0:T(8,128)} %copy-done.5, ...), custom_call_target="tpu_custom_call" | custom-call | tf_op jit(solution)/shard_map/assemble/pallas_call | solution.py:97
  32.3 10.2 %all-to-all-start = ((f32[32,160,128]{2,1,0:T(8,128)}), f32[32,160,128]{2,1,0:T(8,128)S(1)}, u32[]{:S(2)}, u32[]{:S(2)}) async-start(f32[32,160,128]{2,1,0:T(8,128)} %bitcast.19), calls=%async_computation | async-start | bytes 5242880 | tf_op jit(solution)/shard_map/all_to_all | solution.py:242
  42.5 5.9 %pack.7 = (f32[8,192,128]{2,1,0:T(8,128)}, f32[8,192,128]{2,1,0:T(8,128)}, f32[8,192,128]{2,1,0:T(8,128)}, f32[8,192,128]{2,1,0:T(8,128)}) custom-call(f32[128,16384]{1,0:T(8,128)} %x_ref.7), custom_call_target="tpu_custom_call" | custom-call | tf_op jit(solution)/shard_map/pack/pallas_call | solution.py:74
  48.4 0.2 collective-permute-start.12
  48.7 3.0 %collective-permute-start.13 = (f32[8,192,128]{2,1,0:T(8,128)}, f32[8,192,128]{2,1,0:T(8,128)}, u32[]{:S(2)}, u32[]{:S(2)}) collective-permute-start(f32[8,192,128]{2,1,0:T(8,128)} %get-tuple-element.42), channel_id=1, source_target_pairs={{0,6},{1,7},{2,4},{3,5},{4,2},{5,3},{6,0},{7,1},{8,14},{9,15},{10,... | collective-permute-start | bytes 2359304 | tf_op jit(solution)/shard_map/ppermute | solution.py:224
  51.7 0.1 collective-permute-start.14
  51.8 5.7 %pack.6 = (f32[8,192,128]{2,1,0:T(8,128)}, f32[8,192,128]{2,1,0:T(8,128)}, f32[8,192,128]{2,1,0:T(8,128)}, f32[8,192,128]{2,1,0:T(8,128)}) custom-call(f32[128,16384]{1,0:T(8,128)} %x_ref.7), custom_call_target="tpu_custom_call" | custom-call | tf_op jit(solution)/shard_map/pack/pallas_call | solution.py:74
  57.5 0.3 collective-permute-start.9
  57.9 0.0 collective-permute-start.10
  57.9 0.0 collective-permute-done.12.refs_5_
  57.9 1.8 collective-permute-start.11
  59.7 32.3 %collective-permute-done.13.refs_6_ = f32[8,192,128]{2,1,0:T(8,128)} collective-permute-done((f32[8,192,128]{2,1,0:T(8,128)}, f32[8,192,128]{2,1,0:T(8,128)}, u32[]{:S(2)}, u32[]{:S(2)}) %collective-permute-start.13) | collective-permute-done | bytes 786464 | tf_op jit(solution)/shard_map/ppermute | solution.py:224
  92.0 16.9 %collective-permute-done.14.refs_7_ = f32[8,192,128]{2,1,0:T(8,128)} collective-permute-done((f32[8,192,128]{2,1,0:T(8,128)}, f32[8,192,128]{2,1,0:T(8,128)}, u32[]{:S(2)}, u32[]{:S(2)}) %collective-permute-start.14) | collective-permute-done | bytes 786464 | tf_op jit(solution)/shard_map/ppermute | solution.py:224
  108.9 1.5 collective-permute-done.11.refs_3_
  110.3 7.8 %assemble.3 = f32[4,8,384,128]{3,2,1,0:T(8,128)} custom-call(f32[8,192,128]{2,1,0:T(8,128)} %get-tuple-element.36.refs_0_, f32[8,192,128]{2,1,0:T(8,128)} %collective-permute-done.9.refs_1_, f32[8,192,128]{2,1,0:T(8,128)} %collective-permute-done.10.refs_2_, f32[8,192,128]{2,1,0:T(8,128)} %collective-permute-done.11.refs_3_, ...), custom_call_target="tpu_custom_call" | custom-call | tf_op jit(solution)/shard_map/assemble/pallas_call | solution.py:97
  118.2 0.0 all-to-all-done.got_ref
  118.2 0.0 copy-start.8
  118.2 6.2 %all-to-all-start.1 = ((f32[32,384,128]{2,1,0:T(8,128)}), f32[32,384,128]{2,1,0:T(8,128)}, u32[]{:S(2)}, u32[]{:S(2)}) async-start(f32[32,384,128]{2,1,0:T(8,128)} %bitcast.18), calls=%async_computation.1 | async-start | bytes 12582912 | tf_op jit(solution)/shard_map/all_to_all | solution.py:242
  124.5 1.2 collective-permute-start.6
  125.7 81.6 %collective-permute-done.6 = f32[8,1024]{1,0:T(8,128)S(1)} collective-permute-done((f32[8,1024]{1,0:T(8,128)S(1)}, f32[8,1024]{1,0:T(8,128)S(1)}, u32[]{:S(2)}, u32[]{:S(2)}) %collective-permute-start.6) | collective-permute-done | bytes 32800 | tf_op jit(solution)/shard_map/ppermute | solution.py:203
  207.3 1.6 collective-permute-start.7
  209.0 2.1 collective-permute-done.7
  211.0 0.1 collective-permute-start.8
  211.2 5.3 %collective-permute-done.8 = f32[32,1024]{1,0:T(8,128)S(1)} collective-permute-done((f32[32,1024]{1,0:T(8,128)S(1)}, f32[32,1024]{1,0:T(8,128)S(1)}, u32[]{:S(2)}, u32[]{:S(2)}) %collective-permute-start.8) | collective-permute-done | bytes 131104 | tf_op jit(solution)/shard_map/ppermute | solution.py:203
  216.5 0.7 pad_maximum_fusion.4.right_ref
  217.2 0.8 pad_maximum_fusion.1.right_ref
  218.0 0.6 reshape.80
  218.6 0.6 copy.16
  219.2 0.4 reshape.81
  219.6 0.3 copy.13
  220.0 0.3 copy.12
  220.3 0.1 fusion.2
  220.5 1.7 pad_maximum_fusion.left_ref
  222.1 7.3 %correct.2 = (f32[2048,256]{1,0:T(8,128)}, f32[8,8,256]{2,1,0:T(8,128)}, f32[8,256]{1,0:T(8,128)}) custom-call(f32[32,160,128]{2,1,0:T(8,128)} %copy-done, bf16[2048,256]{1,0:T(8,128)(2,1)} %pad_maximum_fusion.left_ref, bf16[256,256]{1,0:T(8,128)(2,1)} %pad_maximum_fusion.4.right_ref), custom_call_target="tpu_custom_call" | custom-call | tf_op jit(solution)/shard_map/correct/pallas_call | solution.py:141
  229.5 0.7 reduce_sum.28
  230.2 9.3 %correct.3 = (f32[2048,768]{1,0:T(8,128)}, f32[8,8,256]{2,1,0:T(8,128)}, f32[8,768]{1,0:T(8,128)}) custom-call(f32[32,384,128]{2,1,0:T(8,128)} %all-to-all-done.1.got_ref, bf16[2048,256]{1,0:T(8,128)(2,1)} %pad_maximum_fusion.left_ref, bf16[256,768]{1,0:T(8,128)(2,1)} %pad_maximum_fusion.1.right_ref), custom_call_target="tpu_custom_call" | custom-call | tf_op jit(solution)/shard_map/correct/pallas_call | solution.py:141
  239.5 0.8 reduce_sum.29
  240.3 1.4 collective-permute-start.15
  241.7 1.1 collective-permute-done.15
  242.8 1.9 collective-permute-start.16
  244.7 1.0 collective-permute-done.16
  245.7 0.7 collective-permute-start.17
  246.4 0.9 slice_add_fusion
  247.3 0.7 broadcast_in_dim.2
  247.9 28.6 %all-to-all-start.2 = ((f32[16,16,128]{2,1,0:T(8,128)}), f32[16,16,128]{2,1,0:T(8,128)S(1)}, u32[]{:S(2)}, u32[]{:S(2)}) async-start(f32[16,16,128]{2,1,0:T(8,128)} %broadcast_in_dim.2), calls=%async_computation.2 | async-start | bytes 262144 | tf_op jit(solution)/shard_map/all_to_all | solution.py:218
  276.5 0.6 sqrt_rsqrt_fusion.1
  277.2 7.0 %all-to-all-done.2 = f32[16,16,128]{2,1,0:T(8,128)S(1)} async-done(((f32[16,16,128]{2,1,0:T(8,128)}), f32[16,16,128]{2,1,0:T(8,128)S(1)}, u32[]{:S(2)}, u32[]{:S(2)}) %all-to-all-start.2) | async-done | bytes 131104 | tf_op jit(solution)/shard_map/all_to_all | solution.py:218
  284.2 0.6 sqrt_rsqrt_fusion
  284.8 9.2 %scale.1 = f32[2048,1024]{1,0:T(8,128)} custom-call(f32[2048,256]{1,0:T(8,128)} %get-tuple-element.35.refs_0_, f32[2048,768]{1,0:T(8,128)} %get-tuple-element.44.refs_1_, f32[8,1,256]{2,1,0:T(1,128)} %bitcast.21, f32[1,1024]{1,0:T(1,128)} %bitcast.23), custom_call_target="tpu_custom_call" | custom-call | tf_op jit(solution)/shard_map/scale/pallas_call | solution.py:177
  (33 shorter events, 0.2 us)
Async XLA Ops:
  2.2 6.0 %copy-start.10 = (f32[8,64,128]{2,1,0:T(8,128)S(1)}, f32[8,64,128]{2,1,0:T(8,128)}, u32[]{:S(2)}) copy-start(f32[8,64,128]{2,1,0:T(8,128)} %get-tuple-element.33) | copy-start | bytes 786436
  2.2 9.9 %copy-start.9 = (f32[8,64,128]{2,1,0:T(8,128)S(1)}, f32[8,64,128]{2,1,0:T(8,128)}, u32[]{:S(2)}) copy-start(f32[8,64,128]{2,1,0:T(8,128)} %get-tuple-element.34) | copy-start | bytes 786436
  2.2 9.9 %collective-permute-start.3 = (f32[8,64,128]{2,1,0:T(8,128)}, f32[8,64,128]{2,1,0:T(8,128)S(1)}, u32[]{:S(2)}, u32[]{:S(2)}) collective-permute-start(f32[8,64,128]{2,1,0:T(8,128)} %get-tuple-element.32), channel_id=1, source_target_pairs={{0,1},{1,0},{2,3},{3,2},{4,5},{5,4},{6,7},{7,6},{8,9},{9,8},{10,11... | collective-permute-start | bytes 786440 | tf_op jit(solution)/shard_map/ppermute | solution.py:224
  6.1 18.4 %collective-permute-start = (f32[8,96,128]{2,1,0:T(8,128)}, f32[8,96,128]{2,1,0:T(8,128)S(1)}, u32[]{:S(2)}, u32[]{:S(2)}) collective-permute-start(f32[8,96,128]{2,1,0:T(8,128)} %get-tuple-element.28), channel_id=1, source_target_pairs={{0,1},{1,0},{2,3},{3,2},{4,5},{5,4},{6,7},{7,6},{8,9},{9,8},{10,11... | collective-permute-start | bytes 1179656 | tf_op jit(solution)/shard_map/ppermute | solution.py:224
  6.1 18.4 %collective-permute-start.1 = (f32[8,96,128]{2,1,0:T(8,128)}, f32[8,96,128]{2,1,0:T(8,128)S(1)}, u32[]{:S(2)}, u32[]{:S(2)}) collective-permute-start(f32[8,96,128]{2,1,0:T(8,128)} %get-tuple-element.29), channel_id=1, source_target_pairs={{0,2},{1,3},{2,0},{3,1},{4,6},{5,7},{6,4},{7,5},{8,10},{9,11},{10,... | collective-permute-start | bytes 1179656 | tf_op jit(solution)/shard_map/ppermute | solution.py:224
  7.9 18.0 %collective-permute-start.2 = (f32[8,96,128]{2,1,0:T(8,128)}, f32[8,96,128]{2,1,0:T(8,128)S(1)}, u32[]{:S(2)}, u32[]{:S(2)}) collective-permute-start(f32[8,96,128]{2,1,0:T(8,128)} %get-tuple-element.30), channel_id=1, source_target_pairs={{0,3},{1,2},{2,1},{3,0},{4,7},{5,6},{6,5},{7,4},{8,11},{9,10},{10,... | collective-permute-start | bytes 1179656 | tf_op jit(solution)/shard_map/ppermute | solution.py:224
  8.2 10.7 %collective-permute-start.4 = (f32[8,64,128]{2,1,0:T(8,128)S(1)}, f32[8,64,128]{2,1,0:T(8,128)S(1)}, u32[]{:S(2)}, u32[]{:S(2)}) collective-permute-start(f32[8,64,128]{2,1,0:T(8,128)S(1)} %copy-done.10), channel_id=1, source_target_pairs={{0,6},{1,7},{2,4},{3,5},{4,2},{5,3},{6,0},{7,1},{8,14},{9,15},{10,... | collective-permute-start | bytes 786440 | tf_op jit(solution)/shard_map/ppermute | solution.py:224
  12.1 13.8 %copy-start.5 = (f32[8,64,128]{2,1,0:T(8,128)}, f32[8,64,128]{2,1,0:T(8,128)S(1)}, u32[]{:S(2)}) copy-start(f32[8,64,128]{2,1,0:T(8,128)S(1)} %collective-permute-done.3.refs_5_) | copy-start | bytes 786436
  12.1 12.4 %collective-permute-start.5 = (f32[8,64,128]{2,1,0:T(8,128)S(1)}, f32[8,64,128]{2,1,0:T(8,128)S(1)}, u32[]{:S(2)}, u32[]{:S(2)}) collective-permute-start(f32[8,64,128]{2,1,0:T(8,128)S(1)} %copy-done.9), channel_id=1, source_target_pairs={{0,7},{1,6},{2,5},{3,4},{4,3},{5,2},{6,1},{7,0},{8,15},{9,14},{10,... | collective-permute-start | bytes 786440 | tf_op jit(solution)/shard_map/ppermute | solution.py:224
  18.9 7.0 %copy-start.6 = (f32[8,64,128]{2,1,0:T(8,128)}, f32[8,64,128]{2,1,0:T(8,128)S(1)}, u32[]{:S(2)}) copy-start(f32[8,64,128]{2,1,0:T(8,128)S(1)} %collective-permute-done.4.refs_6_) | copy-start | bytes 786436
  24.5 1.4 copy-start.7
  24.5 1.4 copy-start.2
  24.5 1.4 copy-start.3
  25.9 0.7 copy-start.4
  32.3 85.9 %all-to-all-start = ((f32[32,160,128]{2,1,0:T(8,128)}), f32[32,160,128]{2,1,0:T(8,128)S(1)}, u32[]{:S(2)}, u32[]{:S(2)}) async-start(f32[32,160,128]{2,1,0:T(8,128)} %bitcast.19), calls=%async_computation | async-start | bytes 5242880 | tf_op jit(solution)/shard_map/all_to_all | solution.py:242
  48.4 9.4 %collective-permute-start.12 = (f32[8,192,128]{2,1,0:T(8,128)}, f32[8,192,128]{2,1,0:T(8,128)S(1)}, u32[]{:S(2)}, u32[]{:S(2)}) collective-permute-start(f32[8,192,128]{2,1,0:T(8,128)} %get-tuple-element.41), channel_id=1, source_target_pairs={{0,1},{1,0},{2,3},{3,2},{4,5},{5,4},{6,7},{7,6},{8,9},{9,8},{10,11... | collective-permute-start | bytes 2359304 | tf_op jit(solution)/shard_map/ppermute | solution.py:224
  48.7 43.3 %collective-permute-start.13 = (f32[8,192,128]{2,1,0:T(8,128)}, f32[8,192,128]{2,1,0:T(8,128)}, u32[]{:S(2)}, u32[]{:S(2)}) collective-permute-start(f32[8,192,128]{2,1,0:T(8,128)} %get-tuple-element.42), channel_id=1, source_target_pairs={{0,6},{1,7},{2,4},{3,5},{4,2},{5,3},{6,0},{7,1},{8,14},{9,15},{10,... | collective-permute-start | bytes 2359304 | tf_op jit(solution)/shard_map/ppermute | solution.py:224
  51.7 57.2 %collective-permute-start.14 = (f32[8,192,128]{2,1,0:T(8,128)}, f32[8,192,128]{2,1,0:T(8,128)}, u32[]{:S(2)}, u32[]{:S(2)}) collective-permute-start(f32[8,192,128]{2,1,0:T(8,128)} %get-tuple-element.43), channel_id=1, source_target_pairs={{0,7},{1,6},{2,5},{3,4},{4,3},{5,2},{6,1},{7,0},{8,15},{9,14},{10,... | collective-permute-start | bytes 2359304 | tf_op jit(solution)/shard_map/ppermute | solution.py:224
  57.5 51.3 %collective-permute-start.9 = (f32[8,192,128]{2,1,0:T(8,128)}, f32[8,192,128]{2,1,0:T(8,128)}, u32[]{:S(2)}, u32[]{:S(2)}) collective-permute-start(f32[8,192,128]{2,1,0:T(8,128)} %get-tuple-element.37), channel_id=1, source_target_pairs={{0,1},{1,0},{2,3},{3,2},{4,5},{5,4},{6,7},{7,6},{8,9},{9,8},{10,11... | collective-permute-start | bytes 2359304 | tf_op jit(solution)/shard_map/ppermute | solution.py:224
  57.9 51.0 %collective-permute-start.10 = (f32[8,192,128]{2,1,0:T(8,128)}, f32[8,192,128]{2,1,0:T(8,128)}, u32[]{:S(2)}, u32[]{:S(2)}) collective-permute-start(f32[8,192,128]{2,1,0:T(8,128)} %get-tuple-element.38), channel_id=1, source_target_pairs={{0,2},{1,3},{2,0},{3,1},{4,6},{5,7},{6,4},{7,5},{8,10},{9,11},{10,... | collective-permute-start | bytes 2359304 | tf_op jit(solution)/shard_map/ppermute | solution.py:224
  57.9 52.4 %copy-start.1 = (f32[8,192,128]{2,1,0:T(8,128)}, f32[8,192,128]{2,1,0:T(8,128)S(1)}, u32[]{:S(2)}) copy-start(f32[8,192,128]{2,1,0:T(8,128)S(1)} %collective-permute-done.12.refs_5_) | copy-start | bytes 2359300
  57.9 52.4 %collective-permute-start.11 = (f32[8,192,128]{2,1,0:T(8,128)}, f32[8,192,128]{2,1,0:T(8,128)}, u32[]{:S(2)}, u32[]{:S(2)}) collective-permute-start(f32[8,192,128]{2,1,0:T(8,128)} %get-tuple-element.39), channel_id=1, source_target_pairs={{0,3},{1,2},{2,1},{3,0},{4,7},{5,6},{6,5},{7,4},{8,11},{9,10},{10,... | collective-permute-start | bytes 2359304 | tf_op jit(solution)/shard_map/ppermute | solution.py:224
  118.2 99.8 %copy-start = (f32[32,160,128]{2,1,0:T(8,128)}, f32[32,160,128]{2,1,0:T(8,128)S(1)}, u32[]{:S(2)}) copy-start(f32[32,160,128]{2,1,0:T(8,128)S(1)} %all-to-all-done.got_ref) | copy-start | bytes 7864324
  118.2 6.3 %copy-start.8 = (f32[8,1024]{1,0:T(8,128)S(1)}, f32[8,1024]{1,0:T(8,128)}, u32[]{:S(2)}) copy-start(f32[8,1024]{1,0:T(8,128)} %param.5) | copy-start | bytes 98308
  118.2 112.0 %all-to-all-start.1 = ((f32[32,384,128]{2,1,0:T(8,128)}), f32[32,384,128]{2,1,0:T(8,128)}, u32[]{:S(2)}, u32[]{:S(2)}) async-start(f32[32,384,128]{2,1,0:T(8,128)} %bitcast.18), calls=%async_computation.1 | async-start | bytes 12582912 | tf_op jit(solution)/shard_map/all_to_all | solution.py:242
  124.5 82.9 %collective-permute-start.6 = (f32[8,1024]{1,0:T(8,128)S(1)}, f32[8,1024]{1,0:T(8,128)S(1)}, u32[]{:S(2)}, u32[]{:S(2)}) collective-permute-start(f32[8,1024]{1,0:T(8,128)S(1)} %copy-done.8), channel_id=1, source_target_pairs={{0,16},{16,0},{1,17},{17,1},{2,18},{18,2},{3,19},{19,3},{4,20},{20... | collective-permute-start | bytes 98312 | tf_op jit(solution)/shard_map/ppermute | solution.py:203
  207.3 3.7 %collective-permute-start.7 = (f32[16,1024]{1,0:T(8,128)S(1)}, f32[16,1024]{1,0:T(8,128)S(1)}, u32[]{:S(2)}, u32[]{:S(2)}) collective-permute-start(f32[16,1024]{1,0:T(8,128)S(1)} %maximum_select_fusion.2), channel_id=1, source_target_pairs={{0,32},{32,0},{64,96},{96,64},{1,33},{33,1},{65,97},{97,65},{2,34}... | collective-permute-start | bytes 196616 | tf_op jit(solution)/shard_map/ppermute | solution.py:203
  211.0 5.4 %collective-permute-start.8 = (f32[32,1024]{1,0:T(8,128)S(1)}, f32[32,1024]{1,0:T(8,128)S(1)}, u32[]{:S(2)}, u32[]{:S(2)}) collective-permute-start(f32[32,1024]{1,0:T(8,128)S(1)} %maximum_select_fusion.1), channel_id=1, source_target_pairs={{0,64},{64,0},{32,96},{96,32},{1,65},{65,1},{33,97},{97,33},{2,66}... | collective-permute-start | bytes 393224 | tf_op jit(solution)/shard_map/ppermute | solution.py:203
  240.3 2.5 collective-permute-start.15
  242.8 2.9 collective-permute-start.16
  245.7 30.9 %collective-permute-start.17 = (f32[8,128]{1,0:T(8,128)S(1)}, f32[8,128]{1,0:T(8,128)S(1)}, u32[]{:S(2)}, u32[]{:S(2)}) collective-permute-start(f32[8,128]{1,0:T(8,128)S(1)} %fusion.4), channel_id=1, source_target_pairs={{0,64},{64,0},{32,96},{96,32},{1,65},{65,1},{33,97},{97,33},{2,66}... | collective-permute-start | bytes 12296 | tf_op jit(solution)/shard_map/ppermute | solution.py:211
  247.9 36.2 %all-to-all-start.2 = ((f32[16,16,128]{2,1,0:T(8,128)}), f32[16,16,128]{2,1,0:T(8,128)S(1)}, u32[]{:S(2)}, u32[]{:S(2)}) async-start(f32[16,16,128]{2,1,0:T(8,128)} %broadcast_in_dim.2), calls=%async_computation.2 | async-start | bytes 262144 | tf_op jit(solution)/shard_map/all_to_all | solution.py:218

commit v2 on v0

v2 whole, which is shorter than its diff:
```python
import functools

import jax
import jax.numpy as jnp
from jax import lax
from jax.experimental import pallas as pl
from jax.experimental.pallas import tpu as pltpu
from jax.sharding import Mesh
from jax.sharding import PartitionSpec as P


ORDER = 16384
TILE = 64
epsilon = 1e-06
F32 = jnp.float32

NAMES = ("y", "xl", "xh", "z1", "z0", "c")
ROWS = ("y", "xl")
COLS = ("xh", "z1", "z0", "c")
SPREAD = ("z0", "c", "xl", "xh", "z1")

CHUNKS = (3, 2, 2, 1)
WIDE = pltpu.CompilerParams(vmem_limit_bytes=56 * 1024 * 1024)
PARAMS = pltpu.CompilerParams(vmem_limit_bytes=24 * 1024 * 1024)


PARTS = 2
RUN = TILE // PARTS


def pack_kernel(count, with_left, *refs):
    out_ref = refs[count + with_left]
    low = lax.broadcasted_iota(jnp.int32, (RUN, 128), 1) < TILE
    for j in range(count):
        rows = slice(j * RUN, j * RUN + RUN)
        for m in range(8):
            xh, z1, z0 = m // 4, m // 2 % 2, m % 2
            a = refs[j][:, m * 128 : m * 128 + 128]
            b = refs[j][:, 1024 + m * 128 : 1024 + m * 128 + 128]
            out_ref[z0 * 2, 0, xh * 2 + z1, rows, :] = jnp.where(low, a, pltpu.roll(b, 64, 1))
            out_ref[z0 * 2 + 1, 0, xh * 2 + z1, rows, :] = jnp.where(low, pltpu.roll(a, 64, 1), b)
    if with_left:
        turned_ref = refs[-1]
        r, part = pl.program_id(0), pl.program_id(1)

        @pl.when((r == 0) & (part == 0))
        def _():
            left = refs[count][...]
            turned_ref[...] = jnp.transpose(jnp.concatenate([left, left], 0))

        half = RUN // 2
        at = pl.multiple_of(r * 64 + part * half, half)
        first = turned_ref[pl.ds(at, half), :]
        second = turned_ref[pl.ds(at + 32, half), :]
        packed = jnp.where(low[0:half], first, second)
        for to in range(4):
            for m in range(4):
                out_ref[to, 0, m, count * RUN : count * RUN + half, :] = packed


def pack(x, left, start, count):
    with_left = left is not None
    height = RUN * count + RUN // 2 * with_left
    in_specs = [pl.BlockSpec((RUN, 2048), lambda r, i, s=start + j: (r * PARTS + i, s)) for j in range(count)]
    args = [x] * count
    scratch = []
    if with_left:
        in_specs.append(pl.BlockSpec((64, 128), lambda r, i: (0, 0)))
        args.append(left)
        scratch.append(pltpu.VMEM((128, 128), F32))
    return pl.pallas_call(
        functools.partial(pack_kernel, count, with_left),
        grid=(2, PARTS),
        in_specs=in_specs,
        out_specs=pl.BlockSpec((4, 1, 4, height, 128), lambda r, i: (0, r, 0, i, 0)),
        out_shape=jax.ShapeDtypeStruct((4, 2, 4, height * PARTS, 128), F32),
        scratch_shapes=scratch,
        compiler_params=WIDE,
        name="pack",
    )(*args)


def deal_kernel(y_ref, *refs):
    for d in range(3):
        refs[3 + d][...] = refs[d][0]


def deal(got, y):
    height = got.shape[2]

    def spec(d):
        return pl.BlockSpec((1, 2, height, 128), lambda i, y: (y[0] ^ d, i, 0, 0))

    return pl.pallas_call(
        deal_kernel,
        grid_spec=pltpu.PrefetchScalarGridSpec(
            num_scalar_prefetch=1,
            grid=(4,),
            in_specs=[spec(d) for d in (1, 2, 3)],
            out_specs=[pl.BlockSpec((2, height, 128), lambda i, y: (i, 0, 0))] * 3,
        ),
        out_shape=[jax.ShapeDtypeStruct((8, height, 128), F32)] * 3,
        compiler_params=PARAMS,
        name="deal",
    )(y, got, got, got)


def piece_specs(height):
    return [pl.BlockSpec((1, 2, height, 128), lambda i, y: (y[0], i, 0, 0))] + [
        pl.BlockSpec((2, height, 128), lambda i, y: (i, 0, 0))
    ] * 3


def left_kernel(y_ref, own_ref, *refs):
    out_ref = refs[3]
    low = lax.broadcasted_iota(jnp.int32, (32, 128), 1) < TILE
    step = own_ref.shape[2] // PARTS
    for d in range(4):
        for k in range(2):
            rows = [slice(p * step + step - RUN // 2, p * step + step) for p in range(PARTS)]
            packed = jnp.concatenate([own_ref[0, k, r, :] if d == 0 else refs[d - 1][k, r, :] for r in rows], 0)
            other = pltpu.roll(packed, 64, 1)
            twice = jnp.concatenate([jnp.where(low, packed, other), jnp.where(low, other, packed)], 0)
            high = twice.astype(jnp.bfloat16)
            rest = (twice - high.astype(F32)).astype(jnp.bfloat16)
            to = slice(k * TILE, k * TILE + TILE)
            out_ref[y_ref[0] ^ d, 0, to, 0:128] = high
            out_ref[y_ref[0] ^ d, 0, to, 128:256] = rest


def left_factor(got, pieces, y):
    return pl.pallas_call(
        left_kernel,
        grid_spec=pltpu.PrefetchScalarGridSpec(
            num_scalar_prefetch=1,
            grid=(4,),
            in_specs=piece_specs(got.shape[2]),
            out_specs=pl.BlockSpec((4, 1, 128, 256), lambda i, y: (0, i, 0, 0)),
        ),
        out_shape=jax.ShapeDtypeStruct((4, 4, 128, 256), jnp.bfloat16),
        compiler_params=PARAMS,
        name="left",
    )(y, got, *pieces)


def correct_kernel(lanes, step, y_ref, own_ref, one_ref, two_ref, three_ref, left_ref, right_ref, out_ref, row_ref, col_ref):
    @pl.when(pl.program_id(0) == 0)
    def _():
        col_ref[...] = jnp.zeros_like(col_ref)

    col_acc = [jnp.zeros((8, 128), F32)] * lanes
    for d in range(4):
        home = y_ref[0] ^ d
        product = jnp.dot(left_ref[home, 0], right_ref[...], preferred_element_type=F32)
        row_acc = jnp.zeros((128, 128), F32)
        for j in range(lanes):
            cols = slice(j * 128, j * 128 + 128)
            tiles = []
            for k in range(2):
                for p in range(PARTS):
                    rows = slice(p * step + j * RUN, p * step + j * RUN + RUN)
                    tiles.append(own_ref[0, k, rows, :] if d == 0 else (one_ref, two_ref, three_ref)[d - 1][k, rows, :])
            tile = jnp.concatenate(tiles, 0) + product[:, cols]
            out_ref[home, 0, :, cols] = tile
            square = tile * tile
            row_acc = row_acc + square
            col_acc[j] = col_acc[j] + jnp.sum(square.reshape(16, 8, 128), 0)
        row_ref[home, 0] = jnp.sum(jnp.transpose(row_acc).reshape(16, 8, 128), 0)
    for j in range(lanes):
        col_ref[:, j * 128 : j * 128 + 128] += col_acc[j]


def correct(got, pieces, y, left, right, lanes):
    width = 128 * lanes
    height = got.shape[2]
    part, row, col = pl.pallas_call(
        functools.partial(correct_kernel, lanes, height // PARTS),
        grid_spec=pltpu.PrefetchScalarGridSpec(
            num_scalar_prefetch=1,
            grid=(4,),
            in_specs=piece_specs(height)
            + [
                pl.BlockSpec((4, 1, 128, 256), lambda i, y: (0, i, 0, 0)),
                pl.BlockSpec((256, width), lambda i, y: (0, 0)),
            ],
            out_specs=[
                pl.BlockSpec((4, 1, 128, width), lambda i, y: (0, i, 0, 0)),
                pl.BlockSpec((4, 1, 8, 128), lambda i, y: (0, i, 0, 0)),
                pl.BlockSpec((8, width), lambda i, y: (0, 0)),
            ],
        ),
        out_shape=[
            jax.ShapeDtypeStruct((4, 4, 128, width), F32),
            jax.ShapeDtypeStruct((4, 4, 8, 128), F32),
            jax.ShapeDtypeStruct((8, width), F32),
        ],
        compiler_params=PARAMS,
        name="correct",
    )(y, got, *pieces, left, right)
    return part.reshape(2048, width), row, col


def scale_kernel(widths, *refs):
    n = len(widths)
    row_ref, col_ref, out_ref = refs[n:]
    row = jnp.transpose(jnp.broadcast_to(row_ref[0], (128, 256)))
    at = 0
    for ref, width in zip(refs, widths):
        for j in range(width // 128):
            cols = slice(at, at + 128)
            out_ref[:, cols] = ref[:, j * 128 : j * 128 + 128] * (row * col_ref[:, cols])
            at += 128


def scale(parts, row, col):
    widths = tuple(p.shape[1] for p in parts)
    return pl.pallas_call(
        functools.partial(scale_kernel, widths),
        grid=(8,),
        in_specs=[pl.BlockSpec((256, w), lambda i: (i, 0)) for w in widths]
        + [pl.BlockSpec((1, 1, 256), lambda i: (i, 0, 0)), pl.BlockSpec((1, 1024), lambda i: (0, 0))],
        out_specs=pl.BlockSpec((256, 1024), lambda i: (i, 0)),
        out_shape=jax.ShapeDtypeStruct((2048, 1024), F32),
        compiler_params=PARAMS,
        name="scale",
    )(*parts, row.reshape(8, 1, 256), col.reshape(1, 1024))


def split(x):
    high = lax.reduce_precision(x, 8, 7)
    low = lax.reduce_precision(x - high, 8, 7)
    return high.astype(jnp.bfloat16), low.astype(jnp.bfloat16)


def flip(d):
    return [(i, i ^ d) for i in range(4)]


def gather_right(part):
    other = lax.ppermute(part, "xl", [(0, 1), (1, 0)])
    first = lax.axis_index("xl") == 0
    part = jnp.where(first, jnp.concatenate([part, other]), jnp.concatenate([other, part]))
    others = [part] + [lax.ppermute(part, "y", flip(d)) for d in (1, 2, 3)]
    y = lax.axis_index("y")
    for bit in (1, 2):
        first = (y & bit) == 0
        others = [jnp.where(first, others[d], others[d ^ bit]) for d in range(4)]
    return jnp.concatenate(others)


def sum_by_permutes(part, moves):
    for axis, d in moves:
        n = lax.axis_size(axis)
        part = part + lax.ppermute(part, axis, [(i, i ^ d) for i in range(n)])
    return part


def body(covariance, factor_left, factor_right):
    y = lax.axis_index("y").reshape(1).astype(jnp.int32)
    got, hops = [], []
    start = 0
    for i, n in enumerate(CHUNKS):
        whole = pack(covariance, factor_left if i == 0 else None, start, n)
        height = whole.shape[3]
        out = lax.all_to_all(whole.reshape(32, height, 128), SPREAD, 0, 0, tiled=True)
        got.append(out.reshape(4, 8, height, 128))
        pieces = deal(got[i], y)
        hops.append([lax.ppermute(p, "y", flip(d)) for p, d in zip(pieces, (1, 2, 3))])
        start += n

    panel = gather_right(factor_right)
    high, low = split(panel)
    right = jnp.concatenate([high, low, high, low])
    left = left_factor(got[0], hops[0], y)

    parts, row_parts, col_parts = [], [], []
    start = 0
    for i, n in enumerate(CHUNKS):
        part, row, col = correct(got[i], hops[i], y, left, right[:, start * 128 : (start + n) * 128], n)
        parts.append(part)
        row_parts.append(row)
        col_parts.append(col)
        start += n
    row_part = jnp.sum(sum(row_parts), axis=2).reshape(16, 128)
    col_part = jnp.sum(jnp.concatenate(col_parts, axis=1), axis=0).reshape(8, 128)
    row_total = sum_by_permutes(row_part, (("c", 1), ("z0", 1), ("z1", 1), ("xh", 1))).reshape(2048)
    col_total = sum_by_permutes(col_part, (("xl", 1), ("y", 1), ("y", 2))).reshape(1024)
    row_factor = lax.rsqrt(jnp.sqrt(row_total / ORDER + epsilon))
    col_factor = lax.rsqrt(jnp.sqrt(col_total / ORDER + epsilon))
    return scale(parts, row_factor, col_factor)


def solution(mesh):
    fine = Mesh(mesh.devices.reshape(4, 2, 2, 2, 2, 2), NAMES)
    placed = (P(NAMES, None), P(None, NAMES), P(ROWS, COLS))
    return jax.shard_map(body, mesh=fine, in_specs=placed, out_specs=P(ROWS, COLS), check_vma=False)
```

time: 342 us -> 261 us (0.76)
  waiting for transfers between devices: 219 us -> 155 us
  Pallas kernels: 0 us -> 43.6 us
  local copies, waits for them, and re-layouts: 40.1 us -> 4.57 us
  blocking collectives: 20.9 us -> 0 us
  matrix products: 12 us -> 0 us
  starting transfers between devices: 41.6 us -> 53.2 us
  other arithmetic: 7.22 us -> 1.04 us
    all_to_all x5 -> x4, waiting for transfers between devices: 219 us -> 87.1 us  [body(): lax.all_to_all(whole.reshape(32, height, 128), SPREAD, 0, 0, tiled=True)]
    ppermute x0 -> x23, waiting for transfers between devices: none -> 68.4 us  [the longest x12 64.6 us: body(): lax.ppermute(p, 'y', flip(d))]
    pallas_call x0 -> x14, Pallas kernels: none -> 43.6 us  [the longest x4 16.6 us: pack(): pl.pallas_call(functools.partial(pack_kernel, count, with_left), grid=(2,...]
    ppermute x0 -> x23, starting transfers between devices: none -> 29.9 us  [the longest x12 15.7 us: body(): lax.ppermute(p, 'y', flip(d))]
    all_to_all x2 -> x0, blocking collectives: 20.9 us -> none  [copy_for_each(): lax.all_to_all(jnp.broadcast_to(shard[None], (length, *shard.shape)), axi...]
    all_to_all x5 -> x4, starting transfers between devices: 41.6 us -> 23.3 us  [body(): lax.all_to_all(whole.reshape(32, height, 128), SPREAD, 0, 0, tiled=True)]
    transpose x3 -> x0, local copies, waits for them, and re-layouts: 16.6 us -> none  [the longest x1 8.26 us: deal_columns(): arranged = source.reshape(height, breadth // (TILE * grid_cols), grid_col...]
    dot_general x1 -> x0, matrix products: 12 us -> none  [body(): jnp.dot(left_rows, right_panel, precision=lax.Precision.HIGHEST, preferre...]
  transfers between devices with their start and end apart: 5 -> 27, of which waited for: 3 -> 10; matrix products, arithmetic and copies ran while one was open for 10% -> 0% of each run, Pallas kernels for 0% -> 13%
where the time goes in v2:
time: 261 us; the launch traced here: 258 us
  waiting for transfers between devices  155 us (59%)
  starting transfers between devices  53.2 us (20%)
  Pallas kernels  43.6 us (17%)
  local copies, waits for them, and re-layouts  4.57 us (2%)
    all_to_all x4, waiting for transfers between devices, body(): lax.all_to_all(whole.reshape(32, height, 128), SPREAD, 0, 0, tiled=True)  87.1 us
    ppermute x12, waiting for transfers between devices, body(): lax.ppermute(p, 'y', flip(d))  64.6 us
    all_to_all x4, starting transfers between devices, body(): lax.all_to_all(whole.reshape(32, height, 128), SPREAD, 0, 0, tiled=True)  23.3 us
    pallas_call x4, Pallas kernels, pack(): pl.pallas_call(functools.partial(pack_kernel, count, with_left), grid=(2,...  16.6 us
    ppermute x12, starting transfers between devices, body(): lax.ppermute(p, 'y', flip(d))  15.7 us
    pallas_call x4, Pallas kernels, correct(): pl.pallas_call(functools.partial(correct_kernel, lanes, height // PARTS),...  11.6 us
    ppermute x7, starting transfers between devices, sum_by_permutes(): part = part + lax.ppermute(part, axis, [(i, i ^ d) for i in range(n)])  8.83 us
    pallas_call x4, Pallas kernels, deal(): pl.pallas_call(deal_kernel, grid_spec=pltpu.PrefetchScalarGridSpec(num_sc...  7.3 us
  transfers between devices with their start and end apart: 27, of which 10 were waited for; matrix products, arithmetic and copies ran while one was open for 0% of the time, Pallas kernels for 13%

profile of v2, /device:TPU:1, one launch (start us, length us, event | category | flops | bytes accessed | tf_op | source)
XLA Modules:
  0.0 258.1 jit_solution(1854277406632707446)
XLA Ops:
  0.0 4.1 %pack.5 = f32[4,2,4,128,128]{4,3,2,1,0:T(8,128)} custom-call(f32[128,16384]{1,0:T(8,128)} %refs_0_.7, f32[128,16384]{1,0:T(8,128)} %refs_0_.7), custom_call_target="tpu_custom_call" | custom-call | tf_op jit(solution)/shard_map/pack/pallas_call | solution.py:71
  4.1 9.4 %all-to-all-start.1 = ((f32[32,128,128]{2,1,0:T(8,128)}), f32[32,128,128]{2,1,0:T(8,128)S(1)}, u32[]{:S(2)}, u32[]{:S(2)}) async-start(f32[32,128,128]{2,1,0:T(8,128)} %bitcast.40), calls=%async_computation.1 | async-start | bytes 4194304 | tf_op jit(solution)/shard_map/all_to_all | solution.py:265
  13.5 4.1 %pack.6 = f32[4,2,4,128,128]{4,3,2,1,0:T(8,128)} custom-call(f32[128,16384]{1,0:T(8,128)} %refs_0_.7, f32[128,16384]{1,0:T(8,128)} %refs_0_.7), custom_call_target="tpu_custom_call" | custom-call | tf_op jit(solution)/shard_map/pack/pallas_call | solution.py:71
  17.6 25.4 %all-to-all-done.1 = f32[32,128,128]{2,1,0:T(8,128)S(1)} async-done(((f32[32,128,128]{2,1,0:T(8,128)}), f32[32,128,128]{2,1,0:T(8,128)S(1)}, u32[]{:S(2)}, u32[]{:S(2)}) %all-to-all-start.1) | async-done | bytes 2097184 | tf_op jit(solution)/shard_map/all_to_all | solution.py:265
  43.0 1.3 copy-done
  44.3 4.8 %all-to-all-start.2 = ((f32[32,128,128]{2,1,0:T(8,128)}), f32[32,128,128]{2,1,0:T(8,128)S(1)}, u32[]{:S(2)}, u32[]{:S(2)}) async-start(f32[32,128,128]{2,1,0:T(8,128)} %bitcast.39), calls=%async_computation.2 | async-start | bytes 4194304 | tf_op jit(solution)/shard_map/all_to_all | solution.py:265
  49.2 4.8 %pack.4 = f32[4,2,4,224,128]{4,3,2,1,0:T(8,128)} custom-call(f32[128,16384]{1,0:T(8,128)} %refs_0_.7, f32[128,16384]{1,0:T(8,128)} %refs_0_.7, f32[128,16384]{1,0:T(8,128)} %refs_0_.7, f32[64,128]{1,0:T(8,128)} %refs_3_.1), custom_call_target="tpu_custom_call" | custom-call | tf_op jit(solution)/shard_map/pack/pallas_call | solution.py:71
  54.0 24.7 %all-to-all-done.2 = f32[32,128,128]{2,1,0:T(8,128)S(1)} async-done(((f32[32,128,128]{2,1,0:T(8,128)}), f32[32,128,128]{2,1,0:T(8,128)S(1)}, u32[]{:S(2)}, u32[]{:S(2)}) %all-to-all-start.2) | async-done | bytes 2097184 | tf_op jit(solution)/shard_map/all_to_all | solution.py:265
  78.6 4.9 %all-to-all-start = ((f32[32,224,128]{2,1,0:T(8,128)}), f32[32,224,128]{2,1,0:T(8,128)}, u32[]{:S(2)}, u32[]{:S(2)}) async-start(f32[32,224,128]{2,1,0:T(8,128)} %bitcast.38), calls=%async_computation | async-start | bytes 7340032 | tf_op jit(solution)/shard_map/all_to_all | solution.py:265
  83.5 1.6 copy-done.1
  85.1 1.7 deal.5
  86.8 1.3 collective-permute-start.7
  88.1 2.6 %collective-permute-start.8 = (f32[8,128,128]{2,1,0:T(8,128)}, f32[8,128,128]{2,1,0:T(8,128)}, u32[]{:S(2)}, u32[]{:S(2)}) collective-permute-start(f32[8,128,128]{2,1,0:T(8,128)} %get-tuple-element.34), channel_id=1, source_target_pairs={{0,64},{32,96},{64,0},{96,32},{1,65},{33,97},{65,1},{97,33},{2,66}... | collective-permute-start | bytes 1572872 | tf_op jit(solution)/shard_map/ppermute | solution.py:268
  90.7 1.4 collective-permute-start.3
  92.1 3.6 %pack.7 = f32[4,2,4,64,128]{4,3,2,1,0:T(8,128)} custom-call(f32[128,16384]{1,0:T(8,128)} %refs_0_.7), custom_call_target="tpu_custom_call" | custom-call | tf_op jit(solution)/shard_map/pack/pallas_call | solution.py:71
  95.7 37.0 %all-to-all-done = f32[32,224,128]{2,1,0:T(8,128)} async-done(((f32[32,224,128]{2,1,0:T(8,128)}), f32[32,224,128]{2,1,0:T(8,128)}, u32[]{:S(2)}, u32[]{:S(2)}) %all-to-all-start) | async-done | bytes 3670048 | tf_op jit(solution)/shard_map/all_to_all | solution.py:265
  132.8 4.2 %all-to-all-start.3 = ((f32[32,64,128]{2,1,0:T(8,128)}), f32[32,64,128]{2,1,0:T(8,128)S(1)}, u32[]{:S(2)}, u32[]{:S(2)}) async-start(f32[32,64,128]{2,1,0:T(8,128)} %bitcast.41), calls=%async_computation.3 | async-start | bytes 2097152 | tf_op jit(solution)/shard_map/all_to_all | solution.py:265
  137.0 0.0 collective-permute-done.3
  137.0 1.4 collective-permute-start.4
  138.4 2.6 %collective-permute-start.5 = (f32[16,1024]{1,0:T(8,128)S(1)}, f32[16,1024]{1,0:T(8,128)S(1)}, u32[]{:S(2)}, u32[]{:S(2)}) collective-permute-start(f32[16,1024]{1,0:T(8,128)S(1)} %maximum_select_fusion), channel_id=1, source_target_pairs={{0,64},{32,96},{64,0},{96,32},{1,65},{33,97},{65,1},{97,33},{2,66}... | collective-permute-start | bytes 196616 | tf_op jit(solution)/shard_map/ppermute | solution.py:243
  141.0 4.1 %deal.4 = (f32[8,224,128]{2,1,0:T(8,128)}, f32[8,224,128]{2,1,0:T(8,128)}, f32[8,224,128]{2,1,0:T(8,128)}) custom-call(s32[1]{0:T(128)} %bitcast.y_ref, f32[4,8,224,128]{3,2,1,0:T(8,128)} %bitcast.2.refs_0_.refs_1_.refs_2_.own_ref, f32[4,8,224,128]{3,2,1,0:T(8,128)} %bitcast.2.refs_0_.refs_1_.refs_2_.own_ref, ...), custom_call_target="tpu_custom_call" | custom-call | tf_op jit(solution)/shard_map/deal/pallas_call | solution.py:94
  145.1 0.0 collective-permute-done.4
  145.1 0.1 collective-permute-start
  145.2 0.0 collective-permute-done.5
  145.2 3.8 %collective-permute-start.1 = (f32[8,224,128]{2,1,0:T(8,128)}, f32[8,224,128]{2,1,0:T(8,128)}, u32[]{:S(2)}, u32[]{:S(2)}) collective-permute-start(f32[8,224,128]{2,1,0:T(8,128)} %get-tuple-element.30), channel_id=1, source_target_pairs={{0,64},{32,96},{64,0},{96,32},{1,65},{33,97},{65,1},{97,33},{2,66}... | collective-permute-start | bytes 2752520 | tf_op jit(solution)/shard_map/ppermute | solution.py:268
  149.0 0.0 collective-permute-done.6
  149.0 0.0 collective-permute-start.2
  149.0 1.4 deal.6
  150.4 0.8 copy-done.3
  151.2 0.8 copy-done.4
  152.0 2.7 %collective-permute-start.9 = (f32[8,128,128]{2,1,0:T(8,128)}, f32[8,128,128]{2,1,0:T(8,128)}, u32[]{:S(2)}, u32[]{:S(2)}) collective-permute-start(f32[8,128,128]{2,1,0:T(8,128)} %get-tuple-element.35), channel_id=1, source_target_pairs={{0,96},{32,64},{64,32},{96,0},{1,97},{33,65},{65,33},{97,1},{2,98}... | collective-permute-start | bytes 1572872 | tf_op jit(solution)/shard_map/ppermute | solution.py:268
  154.7 47.0 %collective-permute-done.9.three_ref = f32[8,128,128]{2,1,0:T(8,128)} collective-permute-done((f32[8,128,128]{2,1,0:T(8,128)}, f32[8,128,128]{2,1,0:T(8,128)}, u32[]{:S(2)}, u32[]{:S(2)}) %collective-permute-start.9) | collective-permute-done | bytes 524320 | tf_op jit(solution)/shard_map/ppermute | solution.py:268
  201.7 0.0 collective-permute-start.11
  201.7 0.0 collective-permute-done.10.one_ref
  201.7 1.0 collective-permute-start.12
  202.7 0.9 pad_maximum_fusion
  203.6 0.1 deal.7
  203.7 0.0 collective-permute-done.refs_0_.one_ref
  203.7 1.8 collective-permute-start.13
  205.5 0.0 collective-permute-done.1.refs_1_.two_ref
  205.5 1.2 collective-permute-start.14
  206.7 0.0 collective-permute-done.2.refs_2_.three_ref
  206.7 1.3 collective-permute-start.15
  208.1 3.1 %left.1.left_ref = bf16[4,4,128,256]{3,2,1,0:T(8,128)(2,1)S(1)} custom-call(s32[1]{0:T(128)} %bitcast.y_ref, f32[4,8,224,128]{3,2,1,0:T(8,128)} %bitcast.2.refs_0_.refs_1_.refs_2_.own_ref, f32[8,224,128]{2,1,0:T(8,128)} %collective-permute-done.refs_0_.one_ref, f32[8,224,128]{2,1,0:T(8,128)} %collective-permute-done.1.refs_1_.two_ref, ...), custom_call_target="tpu_custom_call" | custom-call | tf_op jit(solution)/shard_map/left/pallas_call | solution.py:132
  211.2 3.9 %correct.4 = (f32[4,4,128,384]{3,2,1,0:T(8,128)S(1)}, f32[4,4,8,128]{3,2,1,0:T(8,128)S(1)}, f32[8,384]{1,0:T(8,128)S(1)}) custom-call(s32[1]{0:T(128)} %bitcast.y_ref, f32[4,8,224,128]{3,2,1,0:T(8,128)} %bitcast.2.refs_0_.refs_1_.refs_2_.own_ref, f32[8,224,128]{2,1,0:T(8,128)} %collective-permute-done.refs_0_.one_ref, ...), custom_call_target="tpu_custom_call" | custom-call | tf_op jit(solution)/shard_map/correct/pallas_call | solution.py:176
  215.2 3.2 %correct.5 = (f32[4,4,128,256]{3,2,1,0:T(8,128)S(1)}, f32[4,4,8,128]{3,2,1,0:T(8,128)S(1)}, f32[8,256]{1,0:T(8,128)S(1)}) custom-call(s32[1]{0:T(128)} %bitcast.y_ref, f32[4,8,128,128]{3,2,1,0:T(8,128)S(1)} %bitcast.27, f32[8,128,128]{2,1,0:T(8,128)} %collective-permute-done.7.one_ref, f32[8,128,128]{2,1,0:T(8,128)} %collective-permute-done.8.two_ref, ...), custom_call_target="tpu_custom_call" | custom-call | tf_op jit(solution)/shard_map/correct/pallas_call | solution.py:176
  218.4 15.3 %collective-permute-done.12.three_ref = f32[8,128,128]{2,1,0:T(8,128)} collective-permute-done((f32[8,128,128]{2,1,0:T(8,128)}, f32[8,128,128]{2,1,0:T(8,128)}, u32[]{:S(2)}, u32[]{:S(2)}) %collective-permute-start.12) | collective-permute-done | bytes 524320 | tf_op jit(solution)/shard_map/ppermute | solution.py:268
  233.6 3.1 %correct.6 = (f32[4,4,128,256]{3,2,1,0:T(8,128)S(1)}, f32[4,4,8,128]{3,2,1,0:T(8,128)S(1)}, f32[8,256]{1,0:T(8,128)S(1)}) custom-call(s32[1]{0:T(128)} %bitcast.y_ref, f32[4,8,128,128]{3,2,1,0:T(8,128)S(1)} %bitcast.23, f32[8,128,128]{2,1,0:T(8,128)} %collective-permute-done.10.one_ref, f32[8,128,128]{2,1,0:T(8,128)} %collective-permute-done.11.two_ref, ...), custom_call_target="tpu_custom_call" | custom-call | tf_op jit(solution)/shard_map/correct/pallas_call | solution.py:176
  236.8 0.0 collective-permute-done.14.two_ref
  236.8 2.3 collective-permute-done.15.three_ref
  239.2 1.4 correct.7
  240.6 0.9 collective-permute-start.16
  241.4 1.3 collective-permute-start.20
  242.7 0.0 collective-permute-done.16
  242.7 1.3 collective-permute-start.17
  244.0 1.2 collective-permute-done.17
  245.2 2.7 %collective-permute-start.18 = (f32[16,128]{1,0:T(8,128)S(1)}, f32[16,128]{1,0:T(8,128)S(1)}, u32[]{:S(2)}, u32[]{:S(2)}) collective-permute-start(f32[16,128]{1,0:T(8,128)S(1)} %add.62), channel_id=1, source_target_pairs={{0,4},{4,0},{1,5},{5,1},{2,6},{6,2},{3,7},{7,3},{8,12},{12,8},{9,1... | collective-permute-start | bytes 24584 | tf_op jit(solution)/shard_map/ppermute | solution.py:254
  247.9 0.0 collective-permute-done.21
  247.9 0.3 collective-permute-start.22
  248.2 1.0 collective-permute-done.18
  249.2 2.4 collective-permute-start.19
  251.6 0.3 collective-permute-done.22
  251.9 1.3 collective-permute-done.19
  253.2 4.9 %scale.1 = f32[2048,1024]{1,0:T(8,128)} custom-call(f32[2048,384]{1,0:T(8,128)S(1)} %bitcast.32, f32[2048,256]{1,0:T(8,128)S(1)} %bitcast.33, f32[2048,256]{1,0:T(8,128)S(1)} %bitcast.34, f32[2048,128]{1,0:T(8,128)S(1)} %bitcast.35, f32[8,1,256]{2,1,0:T(1,128)S(1)} %bitcast.36, f32[1,1024]{1,0:T(1,128)S(1)} %bitcast.37), custom_call_target="tpu_custom_call" | custom-call | tf_op jit(solution)/shard_map/scale/pallas_call | solution.py:217
  (34 shorter events, 0.2 us)
Async XLA Ops:
  4.1 38.9 %all-to-all-start.1 = ((f32[32,128,128]{2,1,0:T(8,128)}), f32[32,128,128]{2,1,0:T(8,128)S(1)}, u32[]{:S(2)}, u32[]{:S(2)}) async-start(f32[32,128,128]{2,1,0:T(8,128)} %bitcast.40), calls=%async_computation.1 | async-start | bytes 4194304 | tf_op jit(solution)/shard_map/all_to_all | solution.py:265
  43.0 1.3 copy-start
  44.3 34.3 %all-to-all-start.2 = ((f32[32,128,128]{2,1,0:T(8,128)}), f32[32,128,128]{2,1,0:T(8,128)S(1)}, u32[]{:S(2)}, u32[]{:S(2)}) async-start(f32[32,128,128]{2,1,0:T(8,128)} %bitcast.39), calls=%async_computation.2 | async-start | bytes 4194304 | tf_op jit(solution)/shard_map/all_to_all | solution.py:265
  78.6 54.1 %all-to-all-start = ((f32[32,224,128]{2,1,0:T(8,128)}), f32[32,224,128]{2,1,0:T(8,128)}, u32[]{:S(2)}, u32[]{:S(2)}) async-start(f32[32,224,128]{2,1,0:T(8,128)} %bitcast.38), calls=%async_computation | async-start | bytes 7340032 | tf_op jit(solution)/shard_map/all_to_all | solution.py:265
  83.5 1.6 copy-start.1
  85.1 5.6 %copy-start.6 = (f32[8,1024]{1,0:T(8,128)S(1)}, f32[8,1024]{1,0:T(8,128)}, u32[]{:S(2)}) copy-start(f32[8,1024]{1,0:T(8,128)} %param.5) | copy-start | bytes 98308
  86.8 65.2 %collective-permute-start.7 = (f32[8,128,128]{2,1,0:T(8,128)}, f32[8,128,128]{2,1,0:T(8,128)}, u32[]{:S(2)}, u32[]{:S(2)}) collective-permute-start(f32[8,128,128]{2,1,0:T(8,128)} %get-tuple-element.33), channel_id=1, source_target_pairs={{0,32},{32,0},{64,96},{96,64},{1,33},{33,1},{65,97},{97,65},{2,34}... | collective-permute-start | bytes 1572872 | tf_op jit(solution)/shard_map/ppermute | solution.py:268
  88.1 66.6 %collective-permute-start.8 = (f32[8,128,128]{2,1,0:T(8,128)}, f32[8,128,128]{2,1,0:T(8,128)}, u32[]{:S(2)}, u32[]{:S(2)}) collective-permute-start(f32[8,128,128]{2,1,0:T(8,128)} %get-tuple-element.34), channel_id=1, source_target_pairs={{0,64},{32,96},{64,0},{96,32},{1,65},{33,97},{65,1},{97,33},{2,66}... | collective-permute-start | bytes 1572872 | tf_op jit(solution)/shard_map/ppermute | solution.py:268
  90.7 46.3 %collective-permute-start.3 = (f32[8,1024]{1,0:T(8,128)S(1)}, f32[8,1024]{1,0:T(8,128)S(1)}, u32[]{:S(2)}, u32[]{:S(2)}) collective-permute-start(f32[8,1024]{1,0:T(8,128)S(1)} %copy-done.6), channel_id=1, source_target_pairs={{0,16},{16,0},{1,17},{17,1},{2,18},{18,2},{3,19},{19,3},{4,20},{20... | collective-permute-start | bytes 98312 | tf_op jit(solution)/shard_map/ppermute | solution.py:240
  132.8 70.8 %all-to-all-start.3 = ((f32[32,64,128]{2,1,0:T(8,128)}), f32[32,64,128]{2,1,0:T(8,128)S(1)}, u32[]{:S(2)}, u32[]{:S(2)}) async-start(f32[32,64,128]{2,1,0:T(8,128)} %bitcast.41), calls=%async_computation.3 | async-start | bytes 2097152 | tf_op jit(solution)/shard_map/all_to_all | solution.py:265
  137.0 8.1 %collective-permute-start.4 = (f32[16,1024]{1,0:T(8,128)S(1)}, f32[16,1024]{1,0:T(8,128)S(1)}, u32[]{:S(2)}, u32[]{:S(2)}) collective-permute-start(f32[16,1024]{1,0:T(8,128)S(1)} %maximum_select_fusion), channel_id=1, source_target_pairs={{0,32},{32,0},{64,96},{96,64},{1,33},{33,1},{65,97},{97,65},{2,34}... | collective-permute-start | bytes 196616 | tf_op jit(solution)/shard_map/ppermute | solution.py:243
  138.4 6.8 %collective-permute-start.5 = (f32[16,1024]{1,0:T(8,128)S(1)}, f32[16,1024]{1,0:T(8,128)S(1)}, u32[]{:S(2)}, u32[]{:S(2)}) collective-permute-start(f32[16,1024]{1,0:T(8,128)S(1)} %maximum_select_fusion), channel_id=1, source_target_pairs={{0,64},{32,96},{64,0},{96,32},{1,65},{33,97},{65,1},{97,33},{2,66}... | collective-permute-start | bytes 196616 | tf_op jit(solution)/shard_map/ppermute | solution.py:243
  141.0 8.0 %collective-permute-start.6 = (f32[16,1024]{1,0:T(8,128)S(1)}, f32[16,1024]{1,0:T(8,128)S(1)}, u32[]{:S(2)}, u32[]{:S(2)}) collective-permute-start(f32[16,1024]{1,0:T(8,128)S(1)} %maximum_select_fusion), channel_id=1, source_target_pairs={{0,96},{32,64},{64,32},{96,0},{1,97},{33,65},{65,33},{97,1},{2,98}... | collective-permute-start | bytes 196616 | tf_op jit(solution)/shard_map/ppermute | solution.py:243
  145.1 58.6 %collective-permute-start = (f32[8,224,128]{2,1,0:T(8,128)}, f32[8,224,128]{2,1,0:T(8,128)}, u32[]{:S(2)}, u32[]{:S(2)}) collective-permute-start(f32[8,224,128]{2,1,0:T(8,128)} %get-tuple-element.29), channel_id=1, source_target_pairs={{0,32},{32,0},{64,96},{96,64},{1,33},{33,1},{65,97},{97,65},{2,34}... | collective-permute-start | bytes 2752520 | tf_op jit(solution)/shard_map/ppermute | solution.py:268
  145.2 60.3 %collective-permute-start.1 = (f32[8,224,128]{2,1,0:T(8,128)}, f32[8,224,128]{2,1,0:T(8,128)}, u32[]{:S(2)}, u32[]{:S(2)}) collective-permute-start(f32[8,224,128]{2,1,0:T(8,128)} %get-tuple-element.30), channel_id=1, source_target_pairs={{0,64},{32,96},{64,0},{96,32},{1,65},{33,97},{65,1},{97,33},{2,66}... | collective-permute-start | bytes 2752520 | tf_op jit(solution)/shard_map/ppermute | solution.py:268
  149.0 57.7 %collective-permute-start.2 = (f32[8,224,128]{2,1,0:T(8,128)}, f32[8,224,128]{2,1,0:T(8,128)}, u32[]{:S(2)}, u32[]{:S(2)}) collective-permute-start(f32[8,224,128]{2,1,0:T(8,128)} %get-tuple-element.31), channel_id=1, source_target_pairs={{0,96},{32,64},{64,32},{96,0},{1,97},{33,65},{65,33},{97,1},{2,98}... | collective-permute-start | bytes 2752520 | tf_op jit(solution)/shard_map/ppermute | solution.py:268
  150.4 0.8 copy-start.3
  151.2 0.8 copy-start.4
  152.0 49.7 %collective-permute-start.9 = (f32[8,128,128]{2,1,0:T(8,128)}, f32[8,128,128]{2,1,0:T(8,128)}, u32[]{:S(2)}, u32[]{:S(2)}) collective-permute-start(f32[8,128,128]{2,1,0:T(8,128)} %get-tuple-element.35), channel_id=1, source_target_pairs={{0,96},{32,64},{64,32},{96,0},{1,97},{33,65},{65,33},{97,1},{2,98}... | collective-permute-start | bytes 1572872 | tf_op jit(solution)/shard_map/ppermute | solution.py:268
  154.7 47.0 %collective-permute-start.10 = (f32[8,128,128]{2,1,0:T(8,128)}, f32[8,128,128]{2,1,0:T(8,128)}, u32[]{:S(2)}, u32[]{:S(2)}) collective-permute-start(f32[8,128,128]{2,1,0:T(8,128)} %get-tuple-element.37), channel_id=1, source_target_pairs={{0,32},{32,0},{64,96},{96,64},{1,33},{33,1},{65,97},{97,65},{2,34}... | collective-permute-start | bytes 1572872 | tf_op jit(solution)/shard_map/ppermute | solution.py:268
  201.7 16.7 %collective-permute-start.11 = (f32[8,128,128]{2,1,0:T(8,128)}, f32[8,128,128]{2,1,0:T(8,128)}, u32[]{:S(2)}, u32[]{:S(2)}) collective-permute-start(f32[8,128,128]{2,1,0:T(8,128)} %copy-done.4), channel_id=1, source_target_pairs={{0,64},{32,96},{64,0},{96,32},{1,65},{33,97},{65,1},{97,33},{2,66}... | collective-permute-start | bytes 1572872 | tf_op jit(solution)/shard_map/ppermute | solution.py:268
  201.7 31.9 %collective-permute-start.12 = (f32[8,128,128]{2,1,0:T(8,128)}, f32[8,128,128]{2,1,0:T(8,128)}, u32[]{:S(2)}, u32[]{:S(2)}) collective-permute-start(f32[8,128,128]{2,1,0:T(8,128)} %copy-done.3), channel_id=1, source_target_pairs={{0,96},{32,64},{64,32},{96,0},{1,97},{33,65},{65,33},{97,1},{2,98}... | collective-permute-start | bytes 1572872 | tf_op jit(solution)/shard_map/ppermute | solution.py:268
  203.6 4.4 %copy-start.5 = (bf16[256,1024]{1,0:T(8,128)(2,1)S(1)}, bf16[256,1024]{1,0:T(8,128)(2,1)}, u32[]{:S(2)}) copy-start(bf16[256,1024]{1,0:T(8,128)(2,1)} %pad_maximum_fusion) | copy-start | bytes 1572868
  203.7 33.1 %collective-permute-start.13 = (f32[8,64,128]{2,1,0:T(8,128)S(1)}, f32[8,64,128]{2,1,0:T(8,128)S(1)}, u32[]{:S(2)}, u32[]{:S(2)}) collective-permute-start(f32[8,64,128]{2,1,0:T(8,128)S(1)} %get-tuple-element.41), channel_id=1, source_target_pairs={{0,32},{32,0},{64,96},{96,64},{1,33},{33,1},{65,97},{97,65},{2,34}... | collective-permute-start | bytes 786440 | tf_op jit(solution)/shard_map/ppermute | solution.py:268
  205.5 31.3 %collective-permute-start.14 = (f32[8,64,128]{2,1,0:T(8,128)S(1)}, f32[8,64,128]{2,1,0:T(8,128)S(1)}, u32[]{:S(2)}, u32[]{:S(2)}) collective-permute-start(f32[8,64,128]{2,1,0:T(8,128)S(1)} %get-tuple-element.42), channel_id=1, source_target_pairs={{0,64},{32,96},{64,0},{96,32},{1,65},{33,97},{65,1},{97,33},{2,66}... | collective-permute-start | bytes 786440 | tf_op jit(solution)/shard_map/ppermute | solution.py:268
  206.7 32.4 %collective-permute-start.15 = (f32[8,64,128]{2,1,0:T(8,128)S(1)}, f32[8,64,128]{2,1,0:T(8,128)S(1)}, u32[]{:S(2)}, u32[]{:S(2)}) collective-permute-start(f32[8,64,128]{2,1,0:T(8,128)S(1)} %get-tuple-element.43), channel_id=1, source_target_pairs={{0,96},{32,64},{64,32},{96,0},{1,97},{33,65},{65,33},{97,1},{2,98}... | collective-permute-start | bytes 786440 | tf_op jit(solution)/shard_map/ppermute | solution.py:268
  211.2 4.0 %copy-start.2 = (f32[32,128,128]{2,1,0:T(8,128)S(1)}, f32[32,128,128]{2,1,0:T(8,128)}, u32[]{:S(2)}) copy-start(f32[32,128,128]{2,1,0:T(8,128)} %copy-done) | copy-start | bytes 6291460
  240.6 2.1 collective-permute-start.16
  241.4 2.6 collective-permute-start.20
  242.7 2.5 collective-permute-start.17
  244.0 3.9 %collective-permute-start.21 = (f32[8,128]{1,0:T(8,128)S(1)}, f32[8,128]{1,0:T(8,128)S(1)}, u32[]{:S(2)}, u32[]{:S(2)}) collective-permute-start(f32[8,128]{1,0:T(8,128)S(1)} %bitcast_add_fusion), channel_id=1, source_target_pairs={{0,32},{32,0},{64,96},{96,64},{1,33},{33,1},{65,97},{97,65},{2,34}... | collective-permute-start | bytes 12296 | tf_op jit(solution)/shard_map/ppermute | solution.py:254
  245.2 4.0 %collective-permute-start.18 = (f32[16,128]{1,0:T(8,128)S(1)}, f32[16,128]{1,0:T(8,128)S(1)}, u32[]{:S(2)}, u32[]{:S(2)}) collective-permute-start(f32[16,128]{1,0:T(8,128)S(1)} %add.62), channel_id=1, source_target_pairs={{0,4},{4,0},{1,5},{5,1},{2,6},{6,2},{3,7},{7,3},{8,12},{12,8},{9,1... | collective-permute-start | bytes 24584 | tf_op jit(solution)/shard_map/ppermute | solution.py:254
  247.9 4.0 %collective-permute-start.22 = (f32[8,128]{1,0:T(8,128)S(1)}, f32[8,128]{1,0:T(8,128)S(1)}, u32[]{:S(2)}, u32[]{:S(2)}) collective-permute-start(f32[8,128]{1,0:T(8,128)S(1)} %fusion.3), channel_id=1, source_target_pairs={{0,64},{32,96},{64,0},{96,32},{1,65},{33,97},{65,1},{97,33},{2,66}... | collective-permute-start | bytes 12296 | tf_op jit(solution)/shard_map/ppermute | solution.py:254
  249.2 4.0 %collective-permute-start.19 = (f32[16,128]{1,0:T(8,128)S(1)}, f32[16,128]{1,0:T(8,128)S(1)}, u32[]{:S(2)}, u32[]{:S(2)}) collective-permute-start(f32[16,128]{1,0:T(8,128)S(1)} %add.63), channel_id=1, source_target_pairs={{0,8},{8,0},{1,9},{9,1},{2,10},{10,2},{3,11},{11,3},{4,12},{12,4},... | collective-permute-start | bytes 24584 | tf_op jit(solution)/shard_map/ppermute | solution.py:254

commit v3 on v2

v3 whole, which is shorter than its diff:
```python
import functools

import jax
import jax.numpy as jnp
from jax import lax
from jax.experimental import pallas as pl
from jax.experimental.pallas import tpu as pltpu
from jax.sharding import Mesh
from jax.sharding import PartitionSpec as P


ORDER = 16384
TILE = 64
epsilon = 1e-06
F32 = jnp.float32

NAMES = ("y", "xl", "xh", "z1", "z0", "c")
ROWS = ("y", "xl")
COLS = ("xh", "z1", "z0", "c")
SPREAD = ("z0", "c", "xl", "xh", "z1")

CHUNKS = (3, 2, 2, 1)
WIDE = pltpu.CompilerParams(vmem_limit_bytes=56 * 1024 * 1024)
PARAMS = pltpu.CompilerParams(vmem_limit_bytes=24 * 1024 * 1024)


PARTS = 1
RUN = TILE // PARTS


def pack_kernel(count, with_left, *refs):
    out_ref = refs[count + with_left]
    low = lax.broadcasted_iota(jnp.int32, (RUN, 128), 1) < TILE
    for j in range(count):
        rows = slice(j * RUN, j * RUN + RUN)
        for m in range(8):
            xh, z1, z0 = m // 4, m // 2 % 2, m % 2
            a = refs[j][:, m * 128 : m * 128 + 128]
            b = refs[j][:, 1024 + m * 128 : 1024 + m * 128 + 128]
            out_ref[z0 * 2, 0, xh * 2 + z1, rows, :] = jnp.where(low, a, pltpu.roll(b, 64, 1))
            out_ref[z0 * 2 + 1, 0, xh * 2 + z1, rows, :] = jnp.where(low, pltpu.roll(a, 64, 1), b)
    if with_left:
        turned_ref = refs[-1]
        r, part = pl.program_id(0), pl.program_id(1)

        @pl.when((r == 0) & (part == 0))
        def _():
            left = refs[count][...]
            turned_ref[...] = jnp.transpose(jnp.concatenate([left, left], 0))

        half = RUN // 2
        at = pl.multiple_of(r * 64 + part * half, half)
        first = turned_ref[pl.ds(at, half), :]
        second = turned_ref[pl.ds(at + 32, half), :]
        packed = jnp.where(low[0:half], first, second)
        for to in range(4):
            for m in range(4):
                out_ref[to, 0, m, count * RUN : count * RUN + half, :] = packed


def pack(x, left, start, count):
    with_left = left is not None
    height = RUN * count + RUN // 2 * with_left
    in_specs = [pl.BlockSpec((RUN, 2048), lambda r, i, s=start + j: (r * PARTS + i, s)) for j in range(count)]
    args = [x] * count
    scratch = []
    if with_left:
        in_specs.append(pl.BlockSpec((64, 128), lambda r, i: (0, 0)))
        args.append(left)
        scratch.append(pltpu.VMEM((128, 128), F32))
    return pl.pallas_call(
        functools.partial(pack_kernel, count, with_left),
        grid=(2, PARTS),
        in_specs=in_specs,
        out_specs=pl.BlockSpec((4, 1, 4, height, 128), lambda r, i: (0, r, 0, i, 0)),
        out_shape=jax.ShapeDtypeStruct((4, 2, 4, height * PARTS, 128), F32),
        scratch_shapes=scratch,
        compiler_params=WIDE,
        name="pack",
    )(*args)


def left_kernel(got_ref, out_ref):
    low = lax.broadcasted_iota(jnp.int32, (32, 128), 1) < TILE
    step = got_ref.shape[2] // PARTS
    for to in range(4):
        for k in range(2):
            rows = [slice(p * step + step - RUN // 2, p * step + step) for p in range(PARTS)]
            packed = jnp.concatenate([got_ref[to, k, r, :] for r in rows], 0)
            other = pltpu.roll(packed, 64, 1)
            twice = jnp.concatenate([jnp.where(low, packed, other), jnp.where(low, other, packed)], 0)
            high = twice.astype(jnp.bfloat16)
            rest = (twice - high.astype(F32)).astype(jnp.bfloat16)
            rows = slice(k * TILE, k * TILE + TILE)
            out_ref[to, 0, rows, 0:128] = high
            out_ref[to, 0, rows, 128:256] = rest


def left_factor(got):
    return pl.pallas_call(
        left_kernel,
        grid=(4,),
        in_specs=[pl.BlockSpec((4, 2, got.shape[2], 128), lambda i: (0, i, 0, 0))],
        out_specs=pl.BlockSpec((4, 1, 128, 256), lambda i: (0, i, 0, 0)),
        out_shape=jax.ShapeDtypeStruct((4, 4, 128, 256), jnp.bfloat16),
        compiler_params=PARAMS,
        name="left",
    )(got)


def correct_kernel(lanes, got_ref, left_ref, right_ref, *refs):
    row_ref, col_ref = refs[4:]
    step = got_ref.shape[2] // PARTS
    y = lax.axis_index("y")

    @pl.when(pl.program_id(0) == 0)
    def _():
        col_ref[...] = jnp.zeros_like(col_ref)

    col_acc = [jnp.zeros((8, 128), F32)] * lanes
    for d in range(4):
        to = y ^ d
        product = jnp.dot(left_ref[to, 0], right_ref[...], preferred_element_type=F32)
        row_acc = jnp.zeros((128, 128), F32)
        for j in range(lanes):
            cols = slice(j * 128, j * 128 + 128)
            tiles = []
            for k in range(2):
                for p in range(PARTS):
                    tiles.append(got_ref[to, k, p * step + j * RUN : p * step + j * RUN + RUN, :])
            tile = jnp.concatenate(tiles, 0) + product[:, cols]
            refs[d][:, cols] = tile
            square = tile * tile
            row_acc = row_acc + square
            col_acc[j] = col_acc[j] + jnp.sum(square.reshape(16, 8, 128), 0)
        row_ref[d, 0] = jnp.sum(jnp.transpose(row_acc).reshape(16, 8, 128), 0)
    for j in range(lanes):
        col_ref[:, j * 128 : j * 128 + 128] += col_acc[j]


def correct(got, left, right, lanes):
    width = 128 * lanes
    *pieces, row, col = pl.pallas_call(
        functools.partial(correct_kernel, lanes),
        grid=(4,),
        in_specs=[
            pl.BlockSpec((4, 2, got.shape[2], 128), lambda i: (0, i, 0, 0)),
            pl.BlockSpec((4, 1, 128, 256), lambda i: (0, i, 0, 0)),
            pl.BlockSpec((256, width), lambda i: (0, 0)),
        ],
        out_specs=[pl.BlockSpec((128, width), lambda i: (i, 0))] * 4
        + [
            pl.BlockSpec((4, 1, 8, 128), lambda i: (0, i, 0, 0)),
            pl.BlockSpec((8, width), lambda i: (0, 0)),
        ],
        out_shape=[jax.ShapeDtypeStruct((512, width), F32)] * 4
        + [
            jax.ShapeDtypeStruct((4, 4, 8, 128), F32),
            jax.ShapeDtypeStruct((8, width), F32),
        ],
        compiler_params=PARAMS,
        name="correct",
    )(got, left, right)
    return pieces, row, col


def scale_kernel(widths, *refs):
    n = len(widths)
    row_ref, col_ref, out_ref = refs[4 * n :]
    y = lax.axis_index("y")
    for d in range(4):
        row = jnp.transpose(jnp.broadcast_to(row_ref[d, 0], (128, 128)))
        at = 0
        for i, width in enumerate(widths):
            for j in range(width // 128):
                cols = slice(at, at + 128)
                out_ref[y ^ d, 0, :, cols] = refs[4 * i + d][:, j * 128 : j * 128 + 128] * (row * col_ref[:, cols])
                at += 128


def scale(chunks, row, col):
    widths = tuple(pieces[0].shape[1] for pieces in chunks)
    out = pl.pallas_call(
        functools.partial(scale_kernel, widths),
        grid=(4,),
        in_specs=[pl.BlockSpec((128, w), lambda i: (i, 0)) for w in widths for _ in range(4)]
        + [pl.BlockSpec((4, 1, 1, 128), lambda i: (0, i, 0, 0)), pl.BlockSpec((1, 1024), lambda i: (0, 0))],
        out_specs=pl.BlockSpec((4, 1, 128, 1024), lambda i: (0, i, 0, 0)),
        out_shape=jax.ShapeDtypeStruct((4, 4, 128, 1024), F32),
        compiler_params=PARAMS,
        name="scale",
    )(*[p for pieces in chunks for p in pieces], row.reshape(4, 4, 1, 128), col.reshape(1, 1024))
    return out.reshape(2048, 1024)


def split(x):
    high = lax.reduce_precision(x, 8, 7)
    low = lax.reduce_precision(x - high, 8, 7)
    return high.astype(jnp.bfloat16), low.astype(jnp.bfloat16)


def flip(d):
    return [(i, i ^ d) for i in range(4)]


def gather_right(part):
    other = lax.ppermute(part, "xl", [(0, 1), (1, 0)])
    first = lax.axis_index("xl") == 0
    part = jnp.where(first, jnp.concatenate([part, other]), jnp.concatenate([other, part]))
    others = [part] + [lax.ppermute(part, "y", flip(d)) for d in (1, 2, 3)]
    y = lax.axis_index("y")
    for bit in (1, 2):
        first = (y & bit) == 0
        others = [jnp.where(first, others[d], others[d ^ bit]) for d in range(4)]
    return jnp.concatenate(others)


def sum_over(part, axes):
    n = lax.axis_size(axes)
    total = part
    for d in range(1, n):
        total = total + lax.ppermute(part, axes, [(i, i ^ d) for i in range(n)])
    return total


def body(covariance, factor_left, factor_right):
    panel = gather_right(factor_right)
    high, low = split(panel)
    right = jnp.concatenate([high, low, high, low])

    chunks, row_parts, col_parts, held = [], [], [], []
    start = 0
    for i, n in enumerate(CHUNKS):
        whole = pack(covariance, factor_left if i == 0 else None, start, n)
        height = whole.shape[3]
        out = lax.all_to_all(whole.reshape(32, height, 128), SPREAD, 0, 0, tiled=True)
        got = out.reshape(4, 8, height, 128)
        if i == 0:
            left = left_factor(got)
        pieces, row, col = correct(got, left, right[:, start * 128 : (start + n) * 128], n)
        held.append(pieces)
        row_parts.append(row)
        col_parts.append(col)
        start += n
        if i == len(CHUNKS) - 2:
            row_early = lax.optimization_barrier(jnp.sum(sum(row_parts), axis=2))
    row_part = row_early + jnp.sum(row_parts[-1], axis=2)
    col_part = jnp.sum(jnp.concatenate(col_parts, axis=1), axis=0).reshape(8, 128)
    rows, col = [row_part[0]], col_part
    for d in (1, 2, 3):
        both = jnp.concatenate([row_part[d], col_part])
        both = lax.ppermute(both, "y", flip(d))
        rows.append(both[:4])
        col = col + both[4:]
    col_total = sum_over(col, "xl")
    row_total = jnp.stack(rows).reshape(16, 128)
    for axes in (("xh", "c"), ("z1", "z0")):
        row_total = sum_over(row_total, axes)
    row_factor = lax.rsqrt(jnp.sqrt(row_total / ORDER + epsilon))
    col_factor = lax.rsqrt(jnp.sqrt(col_total / ORDER + epsilon))
    for pieces in held:
        chunks.append([pieces[0]] + [lax.ppermute(pieces[d], "y", flip(d)) for d in (1, 2, 3)])
    return scale(chunks, row_factor, col_factor)


def solution(mesh):
    fine = Mesh(mesh.devices.reshape(4, 2, 2, 2, 2, 2), NAMES)
    placed = (P(NAMES, None), P(None, NAMES), P(ROWS, COLS))
    return jax.shard_map(body, mesh=fine, in_specs=placed, out_specs=P(ROWS, COLS), check_vma=False)
```

time: 261 us -> 291 us (1.11)
  waiting for transfers between devices: 155 us -> 196 us
  Pallas kernels: 43.6 us -> 30.9 us
  local copies, waits for them, and re-layouts: 4.57 us -> 8.16 us
    ppermute x19 -> x22, waiting for transfers between devices: 68.4 us -> 93.8 us  [the longest x12 80.5 us: body(): lax.ppermute(pieces[d], 'y', flip(d))]
    all_to_all x4, waiting for transfers between devices: 87.1 us -> 97.7 us  [body(): lax.all_to_all(whole.reshape(32, height, 128), SPREAD, 0, 0, tiled=True)]
    pallas_call x10 -> x6, Pallas kernels: 26.9 us -> 18.8 us  [the longest x4 11.8 us: correct(): pl.pallas_call(functools.partial(correct_kernel, lanes), grid=(4,), in_sp...]
    pallas_call x4, Pallas kernels: 16.6 us -> 12 us  [pack(): pl.pallas_call(functools.partial(pack_kernel, count, with_left), grid=(2,...]
    ppermute x3, waiting for transfers between devices: 0.01 us -> 4.35 us  [gather_right(): others = [part] + [lax.ppermute(part, 'y', flip(d)) for d in (1, 2, 3)]]
    unnamed x14 -> x32, local copies, waits for them, and re-layouts: 4.53 us -> 8.11 us
    ppermute x19 -> x22, starting transfers between devices: 24.5 us -> 26.2 us  [the longest x12 11.6 us: body(): lax.ppermute(pieces[d], 'y', flip(d))]
  transfers between devices with their start and end apart: 27 -> 30, of which waited for: 10 -> 16; matrix products, arithmetic and copies ran while one was open for 0% -> 0% of each run, Pallas kernels for 13% -> 7%
where the time goes in v3:
time: 291 us; the launch traced here: 290 us
  waiting for transfers between devices  196 us (67%)
  starting transfers between devices  54.8 us (19%)
  Pallas kernels  30.9 us (11%)
  local copies, waits for them, and re-layouts  8.16 us (3%)
    all_to_all x4, waiting for transfers between devices, body(): lax.all_to_all(whole.reshape(32, height, 128), SPREAD, 0, 0, tiled=True)  97.7 us
    ppermute x12, waiting for transfers between devices, body(): lax.ppermute(pieces[d], 'y', flip(d))  80.5 us
    all_to_all x4, starting transfers between devices, body(): lax.all_to_all(whole.reshape(32, height, 128), SPREAD, 0, 0, tiled=True)  23.7 us
    pallas_call x4, Pallas kernels, pack(): pl.pallas_call(functools.partial(pack_kernel, count, with_left), grid=(2,...  12 us
    pallas_call x4, Pallas kernels, correct(): pl.pallas_call(functools.partial(correct_kernel, lanes), grid=(4,), in_sp...  11.8 us
    ppermute x12, starting transfers between devices, body(): lax.ppermute(pieces[d], 'y', flip(d))  11.6 us
    ppermute x7, starting transfers between devices, sum_over(): total = total + lax.ppermute(part, axes, [(i, i ^ d) for i in range(n)])  11.2 us
    ppermute x7, waiting for transfers between devices, sum_over(): total = total + lax.ppermute(part, axes, [(i, i ^ d) for i in range(n)])  10.1 us
  transfers between devices with their start and end apart: 30, of which 16 were waited for; matrix products, arithmetic and copies ran while one was open for 0% of the time, Pallas kernels for 7%

profile of v3, /device:TPU:1, one launch (start us, length us, event | category | flops | bytes accessed | tf_op | source)
XLA Modules:
  0.0 290.2 jit_solution(6397932445969191821)
XLA Ops:
  0.0 2.9 pack.5
  2.9 9.4 %all-to-all-start.1 = ((f32[32,128,128]{2,1,0:T(8,128)}), f32[32,128,128]{2,1,0:T(8,128)S(1)}, u32[]{:S(2)}, u32[]{:S(2)}) async-start(f32[32,128,128]{2,1,0:T(8,128)} %bitcast.31), calls=%async_computation.1 | async-start | bytes 4194304 | tf_op jit(solution)/shard_map/all_to_all | solution.py:236
  12.3 2.9 %pack.6 = f32[4,2,4,128,128]{4,3,2,1,0:T(8,128)} custom-call(f32[128,16384]{1,0:T(8,128)} %refs_0_.7, f32[128,16384]{1,0:T(8,128)} %refs_0_.7), custom_call_target="tpu_custom_call" | custom-call | tf_op jit(solution)/shard_map/pack/pallas_call | solution.py:71
  15.2 26.6 %all-to-all-done.1 = f32[32,128,128]{2,1,0:T(8,128)S(1)} async-done(((f32[32,128,128]{2,1,0:T(8,128)}), f32[32,128,128]{2,1,0:T(8,128)S(1)}, u32[]{:S(2)}, u32[]{:S(2)}) %all-to-all-start.1) | async-done | bytes 2097184 | tf_op jit(solution)/shard_map/all_to_all | solution.py:236
  41.8 4.9 %all-to-all-start.2 = ((f32[32,128,128]{2,1,0:T(8,128)}), f32[32,128,128]{2,1,0:T(8,128)}, u32[]{:S(2)}, u32[]{:S(2)}) async-start(f32[32,128,128]{2,1,0:T(8,128)} %bitcast.30), calls=%async_computation.2 | async-start | bytes 4194304 | tf_op jit(solution)/shard_map/all_to_all | solution.py:236
  46.7 4.0 %pack.4 = f32[4,2,4,224,128]{4,3,2,1,0:T(8,128)} custom-call(f32[128,16384]{1,0:T(8,128)} %refs_0_.7, f32[128,16384]{1,0:T(8,128)} %refs_0_.7, f32[128,16384]{1,0:T(8,128)} %refs_0_.7, f32[64,128]{1,0:T(8,128)} %refs_3_.1), custom_call_target="tpu_custom_call" | custom-call | tf_op jit(solution)/shard_map/pack/pallas_call | solution.py:71
  50.6 25.6 %all-to-all-done.2 = f32[32,128,128]{2,1,0:T(8,128)} async-done(((f32[32,128,128]{2,1,0:T(8,128)}), f32[32,128,128]{2,1,0:T(8,128)}, u32[]{:S(2)}, u32[]{:S(2)}) %all-to-all-start.2) | async-done | bytes 2097184 | tf_op jit(solution)/shard_map/all_to_all | solution.py:236
  76.2 5.0 %all-to-all-start = ((f32[32,224,128]{2,1,0:T(8,128)}), f32[32,224,128]{2,1,0:T(8,128)}, u32[]{:S(2)}, u32[]{:S(2)}) async-start(f32[32,224,128]{2,1,0:T(8,128)} %bitcast.29), calls=%async_computation | async-start | bytes 7340032 | tf_op jit(solution)/shard_map/all_to_all | solution.py:236
  81.2 1.4 collective-permute-start
  82.6 2.3 pack.7
  84.9 45.5 %all-to-all-done = f32[32,224,128]{2,1,0:T(8,128)} async-done(((f32[32,224,128]{2,1,0:T(8,128)}), f32[32,224,128]{2,1,0:T(8,128)}, u32[]{:S(2)}, u32[]{:S(2)}) %all-to-all-start) | async-done | bytes 3670048 | tf_op jit(solution)/shard_map/all_to_all | solution.py:236
  130.5 4.5 %all-to-all-start.3 = ((f32[32,64,128]{2,1,0:T(8,128)}), f32[32,64,128]{2,1,0:T(8,128)}, u32[]{:S(2)}, u32[]{:S(2)}) async-start(f32[32,64,128]{2,1,0:T(8,128)} %bitcast.32), calls=%async_computation.3 | async-start | bytes 2097152 | tf_op jit(solution)/shard_map/all_to_all | solution.py:236
  135.0 2.8 collective-permute-start.3
  137.8 0.3 collective-permute-start.2
  138.1 0.3 collective-permute-start.1
  138.4 1.8 collective-permute-done.3
  140.3 2.5 collective-permute-done.2
  142.9 0.1 pad_maximum_fusion
  143.0 3.0 %left.1.left_ref = bf16[4,4,128,256]{3,2,1,0:T(8,128)(2,1)S(1)} custom-call(f32[4,8,224,128]{3,2,1,0:T(8,128)} %bitcast.1.got_ref), custom_call_target="tpu_custom_call" | custom-call | tf_op jit(solution)/shard_map/left/pallas_call | solution.py:100
  146.0 3.6 %correct.4 = (f32[512,384]{1,0:T(8,128)S(1)}, f32[512,384]{1,0:T(8,128)S(1)}, f32[512,384]{1,0:T(8,128)S(1)}, f32[512,384]{1,0:T(8,128)S(1)}, f32[4,4,8,128]{3,2,1,0:T(8,128)S(1)}, /*index=5*/f32[8,384]{1,0:T(8,128)S(1)}) custom-call(f32[4,8,224,128]{3,2,1,0:T(8,128)} %bitcast.1.got_ref, bf16[4,4,128,256]{3,2,1,0:T(8,128)(2,1)S(1)} %left.1.left_ref, ...), custom_call_target="tpu_custom_call" | custom-call | tf_op jit(solution)/shard_map/correct/pallas_call | solution.py:143
  149.7 0.0 copy-start
  149.7 0.9 copy-done
  150.6 3.7 %correct.6 = (f32[512,256]{1,0:T(8,128)S(1)}, f32[512,256]{1,0:T(8,128)S(1)}, f32[512,256]{1,0:T(8,128)S(1)}, f32[512,256]{1,0:T(8,128)S(1)}, f32[4,4,8,128]{3,2,1,0:T(8,128)S(1)}, /*index=5*/f32[8,256]{1,0:T(8,128)S(1)}) custom-call(f32[4,8,128,128]{3,2,1,0:T(8,128)} %bitcast.5.got_ref, bf16[4,4,128,256]{3,2,1,0:T(8,128)(2,1)S(1)} %left.1.left_ref, ...), custom_call_target="tpu_custom_call" | custom-call | tf_op jit(solution)/shard_map/correct/pallas_call | solution.py:143
  154.3 0.8 copy-done.2
  155.1 1.6 correct.5
  156.7 0.8 copy-done.4
  157.5 0.8 copy-done.9
  158.3 0.8 copy-done.10
  159.1 0.8 copy-done.12
  160.0 2.9 correct.7
  163.0 0.2 collective-permute-start.16
  163.1 2.3 collective-permute-start.18
  165.5 0.8 collective-permute-start.17
  166.3 0.5 collective-permute-done.18
  166.9 2.6 collective-permute-done.17
  169.5 5.4 %collective-permute-start.21 = (f32[16,128]{1,0:T(8,128)S(1)}, f32[16,128]{1,0:T(8,128)S(1)}, u32[]{:S(2)}, u32[]{:S(2)}) collective-permute-start(f32[16,128]{1,0:T(8,128)S(1)} %bitcast.34), channel_id=1, source_target_pairs={{0,9},{1,8},{8,1},{9,0},{2,11},{3,10},{10,3},{11,2},{4,13},{5,12},... | collective-permute-start | bytes 24584 | tf_op jit(solution)/shard_map/ppermute | solution.py:222
  174.9 0.2 collective-permute-start.20
  175.0 0.2 collective-permute-start.13
  175.3 1.9 collective-permute-start.14
  177.2 0.4 collective-permute-start.10
  177.5 2.5 collective-permute-start.11
  180.1 1.5 collective-permute-start.19
  181.5 0.8 collective-permute-done.19
  182.4 0.3 collective-permute-start.25
  182.6 2.5 collective-permute-done.25
  185.1 2.5 collective-permute-start.24
  187.6 1.6 collective-permute-done.24
  189.1 1.5 collective-permute-start.23
  190.6 2.5 collective-permute-done.23
  193.1 0.1 collective-permute-start.22
  193.2 2.8 collective-permute-done.22
  195.9 0.8 collective-permute-start.15
  196.7 1.9 collective-permute-start.12
  198.6 17.0 %collective-permute-done.15.refs_15_ = f32[512,128]{1,0:T(8,128)S(1)} collective-permute-done((f32[512,128]{1,0:T(8,128)S(1)}, f32[512,128]{1,0:T(8,128)S(1)}, u32[]{:S(2)}, u32[]{:S(2)}) %collective-permute-start.15) | collective-permute-done | bytes 262176 | tf_op jit(solution)/shard_map/ppermute | solution.py:262
  215.6 1.0 collective-permute-start.5
  216.6 2.9 collective-permute-start.6
  219.5 7.4 %collective-permute-done.12.refs_11_ = f32[512,256]{1,0:T(8,128)S(1)} collective-permute-done((f32[512,256]{1,0:T(8,128)}, f32[512,256]{1,0:T(8,128)S(1)}, u32[]{:S(2)}, u32[]{:S(2)}) %collective-permute-start.12) | collective-permute-done | bytes 524320 | tf_op jit(solution)/shard_map/ppermute | solution.py:262
  226.9 40.6 %collective-permute-done.8.refs_6_ = f32[512,256]{1,0:T(8,128)S(1)} collective-permute-done((f32[512,256]{1,0:T(8,128)}, f32[512,256]{1,0:T(8,128)S(1)}, u32[]{:S(2)}, u32[]{:S(2)}) %collective-permute-start.8) | collective-permute-done | bytes 524320 | tf_op jit(solution)/shard_map/ppermute | solution.py:262
  267.5 15.6 %collective-permute-done.9.refs_7_ = f32[512,256]{1,0:T(8,128)S(1)} collective-permute-done((f32[512,256]{1,0:T(8,128)}, f32[512,256]{1,0:T(8,128)S(1)}, u32[]{:S(2)}, u32[]{:S(2)}) %collective-permute-start.9) | collective-permute-done | bytes 524320 | tf_op jit(solution)/shard_map/ppermute | solution.py:262
  283.0 0.0 copy-start.1
  283.0 1.1 copy-done.1
  284.2 1.0 copy-done.3
  285.2 1.0 copy-done.5
  286.2 4.0 %scale.1 = f32[4,4,128,1024]{3,2,1,0:T(8,128)} custom-call(f32[512,384]{1,0:T(8,128)S(1)} %copy-done.1, f32[512,384]{1,0:T(8,128)S(1)} %collective-permute-done.4.refs_1_, f32[512,384]{1,0:T(8,128)S(1)} %collective-permute-done.5.refs_2_, f32[512,384]{1,0:T(8,128)S(1)} %collective-permute-done.6.refs_3_, f32[512,256]{1,0:T(8,128)S(1)} %copy-done.5, ...), custom_call_target="tpu_custom_call" | custom-call | tf_op jit(solution)/shard_map/scale/pallas_call | solution.py:183
  (59 shorter events, 0.4 us)
Async XLA Ops:
  2.9 38.9 %all-to-all-start.1 = ((f32[32,128,128]{2,1,0:T(8,128)}), f32[32,128,128]{2,1,0:T(8,128)S(1)}, u32[]{:S(2)}, u32[]{:S(2)}) async-start(f32[32,128,128]{2,1,0:T(8,128)} %bitcast.31), calls=%async_computation.1 | async-start | bytes 4194304 | tf_op jit(solution)/shard_map/all_to_all | solution.py:236
  41.8 34.4 %all-to-all-start.2 = ((f32[32,128,128]{2,1,0:T(8,128)}), f32[32,128,128]{2,1,0:T(8,128)}, u32[]{:S(2)}, u32[]{:S(2)}) async-start(f32[32,128,128]{2,1,0:T(8,128)} %bitcast.30), calls=%async_computation.2 | async-start | bytes 4194304 | tf_op jit(solution)/shard_map/all_to_all | solution.py:236
  76.2 5.0 %copy-start.15 = (f32[8,1024]{1,0:T(8,128)S(1)}, f32[8,1024]{1,0:T(8,128)}, u32[]{:S(2)}) copy-start(f32[8,1024]{1,0:T(8,128)} %param.5) | copy-start | bytes 98308
  76.2 54.3 %all-to-all-start = ((f32[32,224,128]{2,1,0:T(8,128)}), f32[32,224,128]{2,1,0:T(8,128)}, u32[]{:S(2)}, u32[]{:S(2)}) async-start(f32[32,224,128]{2,1,0:T(8,128)} %bitcast.29), calls=%async_computation | async-start | bytes 7340032 | tf_op jit(solution)/shard_map/all_to_all | solution.py:236
  81.2 53.7 %collective-permute-start = (f32[8,1024]{1,0:T(8,128)S(1)}, f32[8,1024]{1,0:T(8,128)S(1)}, u32[]{:S(2)}, u32[]{:S(2)}) collective-permute-start(f32[8,1024]{1,0:T(8,128)S(1)} %copy-done.15), channel_id=1, source_target_pairs={{0,16},{16,0},{1,17},{17,1},{2,18},{18,2},{3,19},{19,3},{4,20},{20... | collective-permute-start | bytes 98312 | tf_op jit(solution)/shard_map/ppermute | solution.py:207
  130.5 29.5 %all-to-all-start.3 = ((f32[32,64,128]{2,1,0:T(8,128)}), f32[32,64,128]{2,1,0:T(8,128)}, u32[]{:S(2)}, u32[]{:S(2)}) async-start(f32[32,64,128]{2,1,0:T(8,128)} %bitcast.32), calls=%async_computation.3 | async-start | bytes 2097152 | tf_op jit(solution)/shard_map/all_to_all | solution.py:236
  135.0 5.3 %collective-permute-start.3 = (f32[16,1024]{1,0:T(8,128)S(1)}, f32[16,1024]{1,0:T(8,128)S(1)}, u32[]{:S(2)}, u32[]{:S(2)}) collective-permute-start(f32[16,1024]{1,0:T(8,128)S(1)} %maximum_select_fusion), channel_id=1, source_target_pairs={{0,96},{32,64},{64,32},{96,0},{1,97},{33,65},{65,33},{97,1},{2,98}... | collective-permute-start | bytes 196616 | tf_op jit(solution)/shard_map/ppermute | solution.py:210
  137.8 5.0 %collective-permute-start.2 = (f32[16,1024]{1,0:T(8,128)S(1)}, f32[16,1024]{1,0:T(8,128)S(1)}, u32[]{:S(2)}, u32[]{:S(2)}) collective-permute-start(f32[16,1024]{1,0:T(8,128)S(1)} %maximum_select_fusion), channel_id=1, source_target_pairs={{0,64},{32,96},{64,0},{96,32},{1,65},{33,97},{65,1},{97,33},{2,66}... | collective-permute-start | bytes 196616 | tf_op jit(solution)/shard_map/ppermute | solution.py:210
  138.1 4.7 %collective-permute-start.1 = (f32[16,1024]{1,0:T(8,128)S(1)}, f32[16,1024]{1,0:T(8,128)S(1)}, u32[]{:S(2)}, u32[]{:S(2)}) collective-permute-start(f32[16,1024]{1,0:T(8,128)S(1)} %maximum_select_fusion), channel_id=1, source_target_pairs={{0,32},{32,0},{64,96},{96,64},{1,33},{33,1},{65,97},{97,65},{2,34}... | collective-permute-start | bytes 196616 | tf_op jit(solution)/shard_map/ppermute | solution.py:210
  149.7 0.9 copy-start
  150.6 6.1 %copy-start.6 = (f32[512,384]{1,0:T(8,128)}, f32[512,384]{1,0:T(8,128)S(1)}, u32[]{:S(2)}) copy-start(f32[512,384]{1,0:T(8,128)S(1)} %get-tuple-element.32) | copy-start | bytes 2359300
  150.6 9.4 %copy-start.7 = (f32[512,384]{1,0:T(8,128)}, f32[512,384]{1,0:T(8,128)S(1)}, u32[]{:S(2)}) copy-start(f32[512,384]{1,0:T(8,128)S(1)} %get-tuple-element.31) | copy-start | bytes 2359300
  150.6 9.4 %copy-start.8 = (f32[512,384]{1,0:T(8,128)}, f32[512,384]{1,0:T(8,128)S(1)}, u32[]{:S(2)}) copy-start(f32[512,384]{1,0:T(8,128)S(1)} %get-tuple-element.30) | copy-start | bytes 2359300
  154.3 0.8 copy-start.2
  155.1 4.9 %copy-start.11 = (f32[512,256]{1,0:T(8,128)}, f32[512,256]{1,0:T(8,128)S(1)}, u32[]{:S(2)}) copy-start(f32[512,256]{1,0:T(8,128)S(1)} %get-tuple-element.40) | copy-start | bytes 1572868
  155.1 4.9 %copy-start.13 = (f32[512,256]{1,0:T(8,128)}, f32[512,256]{1,0:T(8,128)S(1)}, u32[]{:S(2)}) copy-start(f32[512,256]{1,0:T(8,128)S(1)} %get-tuple-element.39) | copy-start | bytes 1572868
  155.1 4.9 %copy-start.14 = (f32[512,256]{1,0:T(8,128)}, f32[512,256]{1,0:T(8,128)S(1)}, u32[]{:S(2)}) copy-start(f32[512,256]{1,0:T(8,128)S(1)} %get-tuple-element.38) | copy-start | bytes 1572868
  156.7 0.8 copy-start.4
  157.5 0.8 copy-start.9
  158.3 0.8 copy-start.10
  159.1 0.8 copy-start.12
  163.0 3.3 %collective-permute-start.16 = (f32[12,128]{1,0:T(8,128)S(1)}, f32[12,128]{1,0:T(8,128)S(1)}, u32[]{:S(2)}, u32[]{:S(2)}) collective-permute-start(f32[12,128]{1,0:T(8,128)S(1)} %get-tuple-element.65), channel_id=1, source_target_pairs={{0,32},{32,0},{64,96},{96,64},{1,33},{33,1},{65,97},{97,65},{2,34}... | collective-permute-start | bytes 18440 | tf_op jit(solution)/shard_map/ppermute | solution.py:252
  163.1 3.7 %collective-permute-start.18 = (f32[12,128]{1,0:T(8,128)S(1)}, f32[12,128]{1,0:T(8,128)S(1)}, u32[]{:S(2)}, u32[]{:S(2)}) collective-permute-start(f32[12,128]{1,0:T(8,128)S(1)} %get-tuple-element.66), channel_id=1, source_target_pairs={{0,96},{32,64},{64,32},{96,0},{1,97},{33,65},{65,33},{97,1},{2,98}... | collective-permute-start | bytes 18440 | tf_op jit(solution)/shard_map/ppermute | solution.py:252
  165.5 4.0 %collective-permute-start.17 = (f32[12,128]{1,0:T(8,128)S(1)}, f32[12,128]{1,0:T(8,128)S(1)}, u32[]{:S(2)}, u32[]{:S(2)}) collective-permute-start(f32[12,128]{1,0:T(8,128)S(1)} %get-tuple-element.67), channel_id=1, source_target_pairs={{0,64},{32,96},{64,0},{96,32},{1,65},{33,97},{65,1},{97,33},{2,66}... | collective-permute-start | bytes 18440 | tf_op jit(solution)/shard_map/ppermute | solution.py:252
  169.5 8.0 %collective-permute-start.21 = (f32[16,128]{1,0:T(8,128)S(1)}, f32[16,128]{1,0:T(8,128)S(1)}, u32[]{:S(2)}, u32[]{:S(2)}) collective-permute-start(f32[16,128]{1,0:T(8,128)S(1)} %bitcast.34), channel_id=1, source_target_pairs={{0,9},{1,8},{8,1},{9,0},{2,11},{3,10},{10,3},{11,2},{4,13},{5,12},... | collective-permute-start | bytes 24584 | tf_op jit(solution)/shard_map/ppermute | solution.py:222
  174.9 5.2 %collective-permute-start.20 = (f32[16,128]{1,0:T(8,128)S(1)}, f32[16,128]{1,0:T(8,128)S(1)}, u32[]{:S(2)}, u32[]{:S(2)}) collective-permute-start(f32[16,128]{1,0:T(8,128)S(1)} %bitcast.35), channel_id=1, source_target_pairs={{0,8},{1,9},{8,0},{9,1},{2,10},{3,11},{10,2},{11,3},{4,12},{5,13},... | collective-permute-start | bytes 24584 | tf_op jit(solution)/shard_map/ppermute | solution.py:222
  175.0 21.7 %collective-permute-start.13 = (f32[512,128]{1,0:T(8,128)S(1)}, f32[512,128]{1,0:T(8,128)S(1)}, u32[]{:S(2)}, u32[]{:S(2)}) collective-permute-start(f32[512,128]{1,0:T(8,128)S(1)} %get-tuple-element.42), channel_id=1, source_target_pairs={{0,32},{32,0},{64,96},{96,64},{1,33},{33,1},{65,97},{97,65},{2,34}... | collective-permute-start | bytes 786440 | tf_op jit(solution)/shard_map/ppermute | solution.py:262
  175.3 23.4 %collective-permute-start.14 = (f32[512,128]{1,0:T(8,128)S(1)}, f32[512,128]{1,0:T(8,128)S(1)}, u32[]{:S(2)}, u32[]{:S(2)}) collective-permute-start(f32[512,128]{1,0:T(8,128)S(1)} %get-tuple-element.43), channel_id=1, source_target_pairs={{0,64},{32,96},{64,0},{96,32},{1,65},{33,97},{65,1},{97,33},{2,66}... | collective-permute-start | bytes 786440 | tf_op jit(solution)/shard_map/ppermute | solution.py:262
  177.2 38.4 %collective-permute-start.10 = (f32[512,256]{1,0:T(8,128)}, f32[512,256]{1,0:T(8,128)S(1)}, u32[]{:S(2)}, u32[]{:S(2)}) collective-permute-start(f32[512,256]{1,0:T(8,128)} %copy-done.14), channel_id=1, source_target_pairs={{0,32},{32,0},{64,96},{96,64},{1,33},{33,1},{65,97},{97,65},{2,34}... | collective-permute-start | bytes 1572872 | tf_op jit(solution)/shard_map/ppermute | solution.py:262
  177.5 39.1 %collective-permute-start.11 = (f32[512,256]{1,0:T(8,128)}, f32[512,256]{1,0:T(8,128)S(1)}, u32[]{:S(2)}, u32[]{:S(2)}) collective-permute-start(f32[512,256]{1,0:T(8,128)} %copy-done.13), channel_id=1, source_target_pairs={{0,64},{32,96},{64,0},{96,32},{1,65},{33,97},{65,1},{97,33},{2,66}... | collective-permute-start | bytes 1572872 | tf_op jit(solution)/shard_map/ppermute | solution.py:262
  180.1 2.3 collective-permute-start.19
  182.4 2.8 collective-permute-start.25
  185.1 4.0 %collective-permute-start.24 = (f32[16,128]{1,0:T(8,128)S(1)}, f32[16,128]{1,0:T(8,128)S(1)}, u32[]{:S(2)}, u32[]{:S(2)}) collective-permute-start(f32[16,128]{1,0:T(8,128)S(1)} %add_add_fusion), channel_id=1, source_target_pairs={{0,6},{2,4},{4,2},{6,0},{1,7},{3,5},{5,3},{7,1},{8,14},{10,12},{12... | collective-permute-start | bytes 24584 | tf_op jit(solution)/shard_map/ppermute | solution.py:222
  189.1 4.0 %collective-permute-start.23 = (f32[16,128]{1,0:T(8,128)S(1)}, f32[16,128]{1,0:T(8,128)S(1)}, u32[]{:S(2)}, u32[]{:S(2)}) collective-permute-start(f32[16,128]{1,0:T(8,128)S(1)} %add_add_fusion), channel_id=1, source_target_pairs={{0,4},{2,6},{4,0},{6,2},{1,5},{3,7},{5,1},{7,3},{8,12},{10,14},{12... | collective-permute-start | bytes 24584 | tf_op jit(solution)/shard_map/ppermute | solution.py:222
  193.1 2.8 collective-permute-start.22
  195.9 19.7 %collective-permute-start.15 = (f32[512,128]{1,0:T(8,128)S(1)}, f32[512,128]{1,0:T(8,128)S(1)}, u32[]{:S(2)}, u32[]{:S(2)}) collective-permute-start(f32[512,128]{1,0:T(8,128)S(1)} %get-tuple-element.44), channel_id=1, source_target_pairs={{0,96},{32,64},{64,32},{96,0},{1,97},{33,65},{65,33},{97,1},{2,98}... | collective-permute-start | bytes 786440 | tf_op jit(solution)/shard_map/ppermute | solution.py:262
  196.7 30.1 %collective-permute-start.12 = (f32[512,256]{1,0:T(8,128)}, f32[512,256]{1,0:T(8,128)S(1)}, u32[]{:S(2)}, u32[]{:S(2)}) collective-permute-start(f32[512,256]{1,0:T(8,128)} %copy-done.11), channel_id=1, source_target_pairs={{0,96},{32,64},{64,32},{96,0},{1,97},{33,65},{65,33},{97,1},{2,98}... | collective-permute-start | bytes 1572872 | tf_op jit(solution)/shard_map/ppermute | solution.py:262
  198.6 28.2 %collective-permute-start.7 = (f32[512,256]{1,0:T(8,128)}, f32[512,256]{1,0:T(8,128)S(1)}, u32[]{:S(2)}, u32[]{:S(2)}) collective-permute-start(f32[512,256]{1,0:T(8,128)} %copy-done.12), channel_id=1, source_target_pairs={{0,32},{32,0},{64,96},{96,64},{1,33},{33,1},{65,97},{97,65},{2,34}... | collective-permute-start | bytes 1572872 | tf_op jit(solution)/shard_map/ppermute | solution.py:262
  215.6 67.4 %collective-permute-start.4 = (f32[512,384]{1,0:T(8,128)}, f32[512,384]{1,0:T(8,128)S(1)}, u32[]{:S(2)}, u32[]{:S(2)}) collective-permute-start(f32[512,384]{1,0:T(8,128)} %copy-done.8), channel_id=1, source_target_pairs={{0,32},{32,0},{64,96},{96,64},{1,33},{33,1},{65,97},{97,65},{2,34}... | collective-permute-start | bytes 2359304 | tf_op jit(solution)/shard_map/ppermute | solution.py:262
  215.6 67.4 %collective-permute-start.5 = (f32[512,384]{1,0:T(8,128)}, f32[512,384]{1,0:T(8,128)S(1)}, u32[]{:S(2)}, u32[]{:S(2)}) collective-permute-start(f32[512,384]{1,0:T(8,128)} %copy-done.7), channel_id=1, source_target_pairs={{0,64},{32,96},{64,0},{96,32},{1,65},{33,97},{65,1},{97,33},{2,66}... | collective-permute-start | bytes 2359304 | tf_op jit(solution)/shard_map/ppermute | solution.py:262
  216.6 66.4 %collective-permute-start.6 = (f32[512,384]{1,0:T(8,128)}, f32[512,384]{1,0:T(8,128)S(1)}, u32[]{:S(2)}, u32[]{:S(2)}) collective-permute-start(f32[512,384]{1,0:T(8,128)} %copy-done.6), channel_id=1, source_target_pairs={{0,96},{32,64},{64,32},{96,0},{1,97},{33,65},{65,33},{97,1},{2,98}... | collective-permute-start | bytes 2359304 | tf_op jit(solution)/shard_map/ppermute | solution.py:262
  226.8 40.6 %collective-permute-start.8 = (f32[512,256]{1,0:T(8,128)}, f32[512,256]{1,0:T(8,128)S(1)}, u32[]{:S(2)}, u32[]{:S(2)}) collective-permute-start(f32[512,256]{1,0:T(8,128)} %copy-done.10), channel_id=1, source_target_pairs={{0,64},{32,96},{64,0},{96,32},{1,65},{33,97},{65,1},{97,33},{2,66}... | collective-permute-start | bytes 1572872 | tf_op jit(solution)/shard_map/ppermute | solution.py:262
  226.8 56.2 %collective-permute-start.9 = (f32[512,256]{1,0:T(8,128)}, f32[512,256]{1,0:T(8,128)S(1)}, u32[]{:S(2)}, u32[]{:S(2)}) collective-permute-start(f32[512,256]{1,0:T(8,128)} %copy-done.9), channel_id=1, source_target_pairs={{0,96},{32,64},{64,32},{96,0},{1,97},{33,65},{65,33},{97,1},{2,98}... | collective-permute-start | bytes 1572872 | tf_op jit(solution)/shard_map/ppermute | solution.py:262
  283.0 1.1 copy-start.1
  284.2 1.0 copy-start.3
  285.2 1.0 copy-start.5

commit v4 on v3

--- a/solution.py
+++ b/solution.py
@@ -108,7 +108,7 @@
     )(got)
 
 
-def correct_kernel(lanes, got_ref, left_ref, right_ref, *refs):
+def correct_kernel(start, lanes, got_ref, left_ref, right_ref, *refs):
     row_ref, col_ref = refs[4:]
     step = got_ref.shape[2] // PARTS
     y = lax.axis_index("y")
@@ -117,10 +117,11 @@
     def _():
         col_ref[...] = jnp.zeros_like(col_ref)
 
+    right = right_ref[:, start * 128 : (start + lanes) * 128]
     col_acc = [jnp.zeros((8, 128), F32)] * lanes
     for d in range(4):
         to = y ^ d
-        product = jnp.dot(left_ref[to, 0], right_ref[...], preferred_element_type=F32)
+        product = jnp.dot(left_ref[to, 0], right, preferred_element_type=F32)
         row_acc = jnp.zeros((128, 128), F32)
         for j in range(lanes):
             cols = slice(j * 128, j * 128 + 128)
@@ -138,15 +139,15 @@
         col_ref[:, j * 128 : j * 128 + 128] += col_acc[j]
 
 
-def correct(got, left, right, lanes):
+def correct(got, left, right, start, lanes):
     width = 128 * lanes
     *pieces, row, col = pl.pallas_call(
-        functools.partial(correct_kernel, lanes),
+        functools.partial(correct_kernel, start, lanes),
         grid=(4,),
         in_specs=[
             pl.BlockSpec((4, 2, got.shape[2], 128), lambda i: (0, i, 0, 0)),
             pl.BlockSpec((4, 1, 128, 256), lambda i: (0, i, 0, 0)),
-            pl.BlockSpec((256, width), lambda i: (0, 0)),
+            pl.BlockSpec((256, 1024), lambda i: (0, 0)),
         ],
         out_specs=[pl.BlockSpec((128, width), lambda i: (i, 0))] * 4
         + [
@@ -237,7 +238,7 @@
         got = out.reshape(4, 8, height, 128)
         if i == 0:
             left = left_factor(got)
-        pieces, row, col = correct(got, left, right[:, start * 128 : (start + n) * 128], n)
+        pieces, row, col = correct(got, left, right, start, n)
         held.append(pieces)
         row_parts.append(row)
         col_parts.append(col)

time: 291 us -> 309 us (1.062)
  waiting for transfers between devices: 196 us -> 208 us
  local copies, waits for them, and re-layouts: 8.16 us -> 12.5 us
    ppermute x1, waiting for transfers between devices: 0.01 us -> 24 us  [gather_right(): other = lax.ppermute(part, 'xl', [(0, 1), (1, 0)])]
    all_to_all x4, waiting for transfers between devices: 97.7 us -> 85.9 us  [body(): lax.all_to_all(whole.reshape(32, height, 128), SPREAD, 0, 0, tiled=True)]
    unnamed x32 -> x44, local copies, waits for them, and re-layouts: 8.11 us -> 12.5 us
  transfers between devices with their start and end apart: 30 -> 30, of which waited for: 16 -> 17; matrix products, arithmetic and copies ran while one was open for 0% -> 0% of each run, Pallas kernels for 7% -> 6%
where the time goes in v4:
time: 309 us; the launch traced here: 308 us
  waiting for transfers between devices  208 us (67%)
  starting transfers between devices  56.4 us (18%)
  Pallas kernels  29.1 us (9%)
  local copies, waits for them, and re-layouts  12.5 us (4%)
    all_to_all x4, waiting for transfers between devices, body(): lax.all_to_all(whole.reshape(32, height, 128), SPREAD, 0, 0, tiled=True)  85.9 us
    ppermute x12, waiting for transfers between devices, body(): lax.ppermute(pieces[d], 'y', flip(d))  81.3 us
    ppermute x1, waiting for transfers between devices, gather_right(): other = lax.ppermute(part, 'xl', [(0, 1), (1, 0)])  24 us
    all_to_all x4, starting transfers between devices, body(): lax.all_to_all(whole.reshape(32, height, 128), SPREAD, 0, 0, tiled=True)  23.6 us
    ppermute x7, starting transfers between devices, sum_over(): total = total + lax.ppermute(part, axes, [(i, i ^ d) for i in range(n)])  13 us
    unnamed x44, local copies, waits for them, and re-layouts  12.5 us
    pallas_call x4, Pallas kernels, pack(): pl.pallas_call(functools.partial(pack_kernel, count, with_left), grid=(2,...  12.1 us
    ppermute x12, starting transfers between devices, body(): lax.ppermute(pieces[d], 'y', flip(d))  11.6 us
  transfers between devices with their start and end apart: 30, of which 17 were waited for; matrix products, arithmetic and copies ran while one was open for 0% of the time, Pallas kernels for 6%

profile of v4, /device:TPU:1, one launch (start us, length us, event | category | flops | bytes accessed | tf_op | source)
XLA Modules:
  0.0 308.3 jit_solution(17859940009979884306)
XLA Ops:
  0.0 2.3 pack.7
  2.3 9.4 %all-to-all-start.3 = ((f32[32,64,128]{2,1,0:T(8,128)}), f32[32,64,128]{2,1,0:T(8,128)S(1)}, u32[]{:S(2)}, u32[]{:S(2)}) async-start(f32[32,64,128]{2,1,0:T(8,128)} %bitcast.33), calls=%async_computation.3 | async-start | bytes 2097152 | tf_op jit(solution)/shard_map/all_to_all | solution.py:237
  11.7 2.9 pack.6
  14.6 14.3 %all-to-all-done.3 = f32[32,64,128]{2,1,0:T(8,128)S(1)} async-done(((f32[32,64,128]{2,1,0:T(8,128)}), f32[32,64,128]{2,1,0:T(8,128)S(1)}, u32[]{:S(2)}, u32[]{:S(2)}) %all-to-all-start.3) | async-done | bytes 1048608 | tf_op jit(solution)/shard_map/all_to_all | solution.py:237
  28.9 4.8 %all-to-all-start.2 = ((f32[32,128,128]{2,1,0:T(8,128)}), f32[32,128,128]{2,1,0:T(8,128)S(1)}, u32[]{:S(2)}, u32[]{:S(2)}) async-start(f32[32,128,128]{2,1,0:T(8,128)} %bitcast.32), calls=%async_computation.2 | async-start | bytes 4194304 | tf_op jit(solution)/shard_map/all_to_all | solution.py:237
  33.7 4.0 %pack.4 = f32[4,2,4,224,128]{4,3,2,1,0:T(8,128)} custom-call(f32[128,16384]{1,0:T(8,128)} %refs_0_.7, f32[128,16384]{1,0:T(8,128)} %refs_0_.7, f32[128,16384]{1,0:T(8,128)} %refs_0_.7, f32[64,128]{1,0:T(8,128)} %refs_3_.1), custom_call_target="tpu_custom_call" | custom-call | tf_op jit(solution)/shard_map/pack/pallas_call | solution.py:71
  37.6 25.5 %all-to-all-done.2 = f32[32,128,128]{2,1,0:T(8,128)S(1)} async-done(((f32[32,128,128]{2,1,0:T(8,128)}), f32[32,128,128]{2,1,0:T(8,128)S(1)}, u32[]{:S(2)}, u32[]{:S(2)}) %all-to-all-start.2) | async-done | bytes 2097184 | tf_op jit(solution)/shard_map/all_to_all | solution.py:237
  63.1 1.3 copy-done
  64.4 4.9 %all-to-all-start = ((f32[32,224,128]{2,1,0:T(8,128)}), f32[32,224,128]{2,1,0:T(8,128)}, u32[]{:S(2)}, u32[]{:S(2)}) async-start(f32[32,224,128]{2,1,0:T(8,128)} %bitcast.30), calls=%async_computation | async-start | bytes 7340032 | tf_op jit(solution)/shard_map/all_to_all | solution.py:237
  69.3 2.9 pack.5
  72.3 46.1 %all-to-all-done = f32[32,224,128]{2,1,0:T(8,128)} async-done(((f32[32,224,128]{2,1,0:T(8,128)}), f32[32,224,128]{2,1,0:T(8,128)}, u32[]{:S(2)}, u32[]{:S(2)}) %all-to-all-start) | async-done | bytes 3670048 | tf_op jit(solution)/shard_map/all_to_all | solution.py:237
  118.3 4.5 %all-to-all-start.1 = ((f32[32,128,128]{2,1,0:T(8,128)}), f32[32,128,128]{2,1,0:T(8,128)}, u32[]{:S(2)}, u32[]{:S(2)}) async-start(f32[32,128,128]{2,1,0:T(8,128)} %bitcast.31), calls=%async_computation.1 | async-start | bytes 4194304 | tf_op jit(solution)/shard_map/all_to_all | solution.py:237
  122.9 1.4 collective-permute-start
  124.3 24.0 %collective-permute-done = f32[8,1024]{1,0:T(8,128)S(1)} collective-permute-done((f32[8,1024]{1,0:T(8,128)S(1)}, f32[8,1024]{1,0:T(8,128)S(1)}, u32[]{:S(2)}, u32[]{:S(2)}) %collective-permute-start) | collective-permute-done | bytes 32800 | tf_op jit(solution)/shard_map/ppermute | solution.py:208
  148.3 2.8 collective-permute-start.3
  151.8 1.2 collective-permute-done.3
  153.0 2.7 collective-permute-done.2
  155.8 3.0 left.1.left_ref
  158.9 3.8 %correct.4 = (f32[512,384]{1,0:T(8,128)S(1)}, f32[512,384]{1,0:T(8,128)S(1)}, f32[512,384]{1,0:T(8,128)S(1)}, f32[512,384]{1,0:T(8,128)S(1)}, f32[4,4,8,128]{3,2,1,0:T(8,128)S(1)}, /*index=5*/f32[8,384]{1,0:T(8,128)S(1)}) custom-call(f32[4,8,224,128]{3,2,1,0:T(8,128)} %bitcast.1.got_ref, bf16[4,4,128,256]{3,2,1,0:T(8,128)(2,1)S(1)} %left.1.left_ref, ...), custom_call_target="tpu_custom_call" | custom-call | tf_op jit(solution)/shard_map/correct/pallas_call | solution.py:144
  162.7 0.9 copy-done.2
  163.6 1.4 correct.7
  165.0 0.7 copy-done.4
  165.7 0.6 copy-done.6
  166.4 0.7 copy-done.18
  167.0 0.7 copy-done.19
  167.7 0.7 copy-done.20
  168.5 1.6 correct.6
  170.1 0.6 copy-done.7
  170.7 0.8 copy-done.14
  171.5 0.8 copy-done.16
  172.3 0.8 copy-done.17
  173.2 3.2 %correct.5 = (f32[512,256]{1,0:T(8,128)S(1)}, f32[512,256]{1,0:T(8,128)S(1)}, f32[512,256]{1,0:T(8,128)S(1)}, f32[512,256]{1,0:T(8,128)S(1)}, f32[4,4,8,128]{3,2,1,0:T(8,128)S(1)}, /*index=5*/f32[8,256]{1,0:T(8,128)S(1)}) custom-call(f32[4,8,128,128]{3,2,1,0:T(8,128)} %bitcast.3.got_ref, bf16[4,4,128,256]{3,2,1,0:T(8,128)(2,1)S(1)} %left.1.left_ref, ...), custom_call_target="tpu_custom_call" | custom-call | tf_op jit(solution)/shard_map/correct/pallas_call | solution.py:144
  176.3 0.8 copy-done.12
  177.1 0.8 copy-done.13
  177.9 0.8 copy-done.15
  178.7 0.6 copy-done.8
  179.3 0.9 reduce_sum.28
  180.2 0.7 maximum_reduce_fusion
  181.0 2.1 collective-permute-start.18
  183.2 1.1 collective-permute-start.17
  184.3 0.5 collective-permute-done.18
  184.8 2.3 collective-permute-done.17
  187.2 6.2 %collective-permute-start.21 = (f32[16,128]{1,0:T(8,128)S(1)}, f32[16,128]{1,0:T(8,128)S(1)}, u32[]{:S(2)}, u32[]{:S(2)}) collective-permute-start(f32[16,128]{1,0:T(8,128)S(1)} %bitcast.35), channel_id=1, source_target_pairs={{0,9},{1,8},{8,1},{9,0},{2,11},{3,10},{10,3},{11,2},{4,13},{5,12},... | collective-permute-start | bytes 24584 | tf_op jit(solution)/shard_map/ppermute | solution.py:223
  193.4 0.6 collective-permute-start.20
  194.0 1.8 collective-permute-start.14
  196.1 2.9 collective-permute-start.11
  199.0 1.0 collective-permute-start.19
  200.1 0.8 collective-permute-done.19
  201.0 2.6 collective-permute-done.25
  203.6 3.6 %collective-permute-start.24 = (f32[16,128]{1,0:T(8,128)S(1)}, f32[16,128]{1,0:T(8,128)S(1)}, u32[]{:S(2)}, u32[]{:S(2)}) collective-permute-start(f32[16,128]{1,0:T(8,128)S(1)} %add_add_fusion), channel_id=1, source_target_pairs={{0,6},{2,4},{4,2},{6,0},{1,7},{3,5},{5,3},{7,1},{8,14},{10,12},{12... | collective-permute-start | bytes 24584 | tf_op jit(solution)/shard_map/ppermute | solution.py:223
  207.3 1.3 collective-permute-done.24
  208.6 1.4 collective-permute-start.23
  210.0 2.6 collective-permute-done.23
  212.6 2.8 collective-permute-done.22
  215.4 0.6 collective-permute-start.15
  216.0 2.0 collective-permute-start.12
  218.1 17.8 %collective-permute-done.15.refs_15_ = f32[512,128]{1,0:T(8,128)S(1)} collective-permute-done((f32[512,128]{1,0:T(8,128)}, f32[512,128]{1,0:T(8,128)S(1)}, u32[]{:S(2)}, u32[]{:S(2)}) %collective-permute-start.15) | collective-permute-done | bytes 262176 | tf_op jit(solution)/shard_map/ppermute | solution.py:263
  235.9 0.6 collective-permute-start.5
  236.5 3.3 %collective-permute-start.6 = (f32[512,384]{1,0:T(8,128)}, f32[512,384]{1,0:T(8,128)S(1)}, u32[]{:S(2)}, u32[]{:S(2)}) collective-permute-start(f32[512,384]{1,0:T(8,128)} %copy-done.9), channel_id=1, source_target_pairs={{0,96},{32,64},{64,32},{96,0},{1,97},{33,65},{65,33},{97,1},{2,98}... | collective-permute-start | bytes 2359304 | tf_op jit(solution)/shard_map/ppermute | solution.py:263
  239.8 7.4 %collective-permute-done.12.refs_11_ = f32[512,256]{1,0:T(8,128)S(1)} collective-permute-done((f32[512,256]{1,0:T(8,128)}, f32[512,256]{1,0:T(8,128)S(1)}, u32[]{:S(2)}, u32[]{:S(2)}) %collective-permute-start.12) | collective-permute-done | bytes 524320 | tf_op jit(solution)/shard_map/ppermute | solution.py:263
  247.2 39.6 %collective-permute-done.8.refs_6_ = f32[512,256]{1,0:T(8,128)S(1)} collective-permute-done((f32[512,256]{1,0:T(8,128)}, f32[512,256]{1,0:T(8,128)S(1)}, u32[]{:S(2)}, u32[]{:S(2)}) %collective-permute-start.8) | collective-permute-done | bytes 524320 | tf_op jit(solution)/shard_map/ppermute | solution.py:263
  286.8 16.5 %collective-permute-done.9.refs_7_ = f32[512,256]{1,0:T(8,128)S(1)} collective-permute-done((f32[512,256]{1,0:T(8,128)}, f32[512,256]{1,0:T(8,128)S(1)}, u32[]{:S(2)}, u32[]{:S(2)}) %collective-permute-start.9) | collective-permute-done | bytes 524320 | tf_op jit(solution)/shard_map/ppermute | solution.py:263
  303.4 0.9 copy-done.5
  304.3 4.0 %scale.1 = f32[4,4,128,1024]{3,2,1,0:T(8,128)} custom-call(f32[512,384]{1,0:T(8,128)S(1)} %copy-done.3, f32[512,384]{1,0:T(8,128)S(1)} %collective-permute-done.4.refs_1_, f32[512,384]{1,0:T(8,128)S(1)} %collective-permute-done.5.refs_2_, f32[512,384]{1,0:T(8,128)S(1)} %collective-permute-done.6.refs_3_, f32[512,256]{1,0:T(8,128)S(1)} %get-tuple-element.33.refs_4_, ...), custom_call_target="tpu_custom_call" | custom-call | tf_op jit(solution)/shard_map/scale/pallas_call | solution.py:184
  (68 shorter events, 1.5 us)
Async XLA Ops:
  2.3 26.6 %all-to-all-start.3 = ((f32[32,64,128]{2,1,0:T(8,128)}), f32[32,64,128]{2,1,0:T(8,128)S(1)}, u32[]{:S(2)}, u32[]{:S(2)}) async-start(f32[32,64,128]{2,1,0:T(8,128)} %bitcast.33), calls=%async_computation.3 | async-start | bytes 2097152 | tf_op jit(solution)/shard_map/all_to_all | solution.py:237
  28.9 34.3 %all-to-all-start.2 = ((f32[32,128,128]{2,1,0:T(8,128)}), f32[32,128,128]{2,1,0:T(8,128)S(1)}, u32[]{:S(2)}, u32[]{:S(2)}) async-start(f32[32,128,128]{2,1,0:T(8,128)} %bitcast.32), calls=%async_computation.2 | async-start | bytes 4194304 | tf_op jit(solution)/shard_map/all_to_all | solution.py:237
  63.1 1.3 copy-start
  64.4 53.9 %all-to-all-start = ((f32[32,224,128]{2,1,0:T(8,128)}), f32[32,224,128]{2,1,0:T(8,128)}, u32[]{:S(2)}, u32[]{:S(2)}) async-start(f32[32,224,128]{2,1,0:T(8,128)} %bitcast.30), calls=%async_computation | async-start | bytes 7340032 | tf_op jit(solution)/shard_map/all_to_all | solution.py:237
  72.3 50.7 %copy-start.21 = (f32[8,1024]{1,0:T(8,128)S(1)}, f32[8,1024]{1,0:T(8,128)}, u32[]{:S(2)}) copy-start(f32[8,1024]{1,0:T(8,128)} %param.5) | copy-start | bytes 98308
  118.3 54.8 %all-to-all-start.1 = ((f32[32,128,128]{2,1,0:T(8,128)}), f32[32,128,128]{2,1,0:T(8,128)}, u32[]{:S(2)}, u32[]{:S(2)}) async-start(f32[32,128,128]{2,1,0:T(8,128)} %bitcast.31), calls=%async_computation.1 | async-start | bytes 4194304 | tf_op jit(solution)/shard_map/all_to_all | solution.py:237
  122.9 25.4 %collective-permute-start = (f32[8,1024]{1,0:T(8,128)S(1)}, f32[8,1024]{1,0:T(8,128)S(1)}, u32[]{:S(2)}, u32[]{:S(2)}) collective-permute-start(f32[8,1024]{1,0:T(8,128)S(1)} %copy-done.21), channel_id=1, source_target_pairs={{0,16},{16,0},{1,17},{17,1},{2,18},{18,2},{3,19},{19,3},{4,20},{20... | collective-permute-start | bytes 98312 | tf_op jit(solution)/shard_map/ppermute | solution.py:208
  148.3 4.7 %collective-permute-start.3 = (f32[16,1024]{1,0:T(8,128)S(1)}, f32[16,1024]{1,0:T(8,128)S(1)}, u32[]{:S(2)}, u32[]{:S(2)}) collective-permute-start(f32[16,1024]{1,0:T(8,128)S(1)} %maximum_select_fusion), channel_id=1, source_target_pairs={{0,96},{32,64},{64,32},{96,0},{1,97},{33,65},{65,33},{97,1},{2,98}... | collective-permute-start | bytes 196616 | tf_op jit(solution)/shard_map/ppermute | solution.py:211
  151.1 4.6 %collective-permute-start.2 = (f32[16,1024]{1,0:T(8,128)S(1)}, f32[16,1024]{1,0:T(8,128)S(1)}, u32[]{:S(2)}, u32[]{:S(2)}) collective-permute-start(f32[16,1024]{1,0:T(8,128)S(1)} %maximum_select_fusion), channel_id=1, source_target_pairs={{0,64},{32,96},{64,0},{96,32},{1,65},{33,97},{65,1},{97,33},{2,66}... | collective-permute-start | bytes 196616 | tf_op jit(solution)/shard_map/ppermute | solution.py:211
  151.4 4.3 %collective-permute-start.1 = (f32[16,1024]{1,0:T(8,128)S(1)}, f32[16,1024]{1,0:T(8,128)S(1)}, u32[]{:S(2)}, u32[]{:S(2)}) collective-permute-start(f32[16,1024]{1,0:T(8,128)S(1)} %maximum_select_fusion), channel_id=1, source_target_pairs={{0,32},{32,0},{64,96},{96,64},{1,33},{33,1},{65,97},{97,65},{2,34}... | collective-permute-start | bytes 196616 | tf_op jit(solution)/shard_map/ppermute | solution.py:211
  158.9 9.6 %copy-start.1 = (f32[32,128,128]{2,1,0:T(8,128)S(1)}, f32[32,128,128]{2,1,0:T(8,128)}, u32[]{:S(2)}) copy-start(f32[32,128,128]{2,1,0:T(8,128)} %copy-done) | copy-start | bytes 6291460
  162.7 0.9 copy-start.2
  163.6 1.5 copy-start.9
  163.6 4.9 %copy-start.10 = (f32[512,384]{1,0:T(8,128)}, f32[512,384]{1,0:T(8,128)S(1)}, u32[]{:S(2)}) copy-start(f32[512,384]{1,0:T(8,128)S(1)} %get-tuple-element.31) | copy-start | bytes 2359300
  163.6 4.9 %copy-start.11 = (f32[512,384]{1,0:T(8,128)}, f32[512,384]{1,0:T(8,128)S(1)}, u32[]{:S(2)}) copy-start(f32[512,384]{1,0:T(8,128)S(1)} %get-tuple-element.30) | copy-start | bytes 2359300
  165.0 0.7 copy-start.4
  165.7 0.6 copy-start.6
  166.4 0.7 copy-start.18
  167.0 0.7 copy-start.19
  167.7 0.7 copy-start.20
  168.5 134.9 %copy-start.3 = (f32[512,384]{1,0:T(8,128)S(1)}, f32[512,384]{1,0:T(8,128)}, u32[]{:S(2)}) copy-start(f32[512,384]{1,0:T(8,128)} %copy-done.2) | copy-start | bytes 2359300
  170.1 0.6 copy-start.7
  170.7 0.8 copy-start.14
  171.5 0.9 copy-start.16
  172.3 0.8 copy-start.17
  176.3 0.8 copy-start.12
  177.1 0.8 copy-start.13
  177.9 0.8 copy-start.15
  178.7 0.6 copy-start.8
  180.9 3.3 %collective-permute-start.16 = (f32[12,128]{1,0:T(8,128)S(1)}, f32[12,128]{1,0:T(8,128)S(1)}, u32[]{:S(2)}, u32[]{:S(2)}) collective-permute-start(f32[12,128]{1,0:T(8,128)S(1)} %get-tuple-element.63), channel_id=1, source_target_pairs={{0,32},{32,0},{64,96},{96,64},{1,33},{33,1},{65,97},{97,65},{2,34}... | collective-permute-start | bytes 18440 | tf_op jit(solution)/shard_map/ppermute | solution.py:253
  181.0 3.8 %collective-permute-start.18 = (f32[12,128]{1,0:T(8,128)S(1)}, f32[12,128]{1,0:T(8,128)S(1)}, u32[]{:S(2)}, u32[]{:S(2)}) collective-permute-start(f32[12,128]{1,0:T(8,128)S(1)} %get-tuple-element.64), channel_id=1, source_target_pairs={{0,96},{32,64},{64,32},{96,0},{1,97},{33,65},{65,33},{97,1},{2,98}... | collective-permute-start | bytes 18440 | tf_op jit(solution)/shard_map/ppermute | solution.py:253
  183.2 4.0 %collective-permute-start.17 = (f32[12,128]{1,0:T(8,128)S(1)}, f32[12,128]{1,0:T(8,128)S(1)}, u32[]{:S(2)}, u32[]{:S(2)}) collective-permute-start(f32[12,128]{1,0:T(8,128)S(1)} %get-tuple-element.65), channel_id=1, source_target_pairs={{0,64},{32,96},{64,0},{96,32},{1,65},{33,97},{65,1},{97,33},{2,66}... | collective-permute-start | bytes 18440 | tf_op jit(solution)/shard_map/ppermute | solution.py:253
  187.2 8.9 %collective-permute-start.21 = (f32[16,128]{1,0:T(8,128)S(1)}, f32[16,128]{1,0:T(8,128)S(1)}, u32[]{:S(2)}, u32[]{:S(2)}) collective-permute-start(f32[16,128]{1,0:T(8,128)S(1)} %bitcast.35), channel_id=1, source_target_pairs={{0,9},{1,8},{8,1},{9,0},{2,11},{3,10},{10,3},{11,2},{4,13},{5,12},... | collective-permute-start | bytes 24584 | tf_op jit(solution)/shard_map/ppermute | solution.py:223
  193.4 5.6 %collective-permute-start.20 = (f32[16,128]{1,0:T(8,128)S(1)}, f32[16,128]{1,0:T(8,128)S(1)}, u32[]{:S(2)}, u32[]{:S(2)}) collective-permute-start(f32[16,128]{1,0:T(8,128)S(1)} %bitcast.36), channel_id=1, source_target_pairs={{0,8},{1,9},{8,0},{9,1},{2,10},{3,11},{10,2},{11,3},{4,12},{5,13},... | collective-permute-start | bytes 24584 | tf_op jit(solution)/shard_map/ppermute | solution.py:223
  194.0 22.1 %collective-permute-start.13 = (f32[512,128]{1,0:T(8,128)}, f32[512,128]{1,0:T(8,128)S(1)}, u32[]{:S(2)}, u32[]{:S(2)}) collective-permute-start(f32[512,128]{1,0:T(8,128)} %copy-done.20), channel_id=1, source_target_pairs={{0,32},{32,0},{64,96},{96,64},{1,33},{33,1},{65,97},{97,65},{2,34}... | collective-permute-start | bytes 786440 | tf_op jit(solution)/shard_map/ppermute | solution.py:263
  194.0 24.1 %collective-permute-start.14 = (f32[512,128]{1,0:T(8,128)}, f32[512,128]{1,0:T(8,128)S(1)}, u32[]{:S(2)}, u32[]{:S(2)}) collective-permute-start(f32[512,128]{1,0:T(8,128)} %copy-done.19), channel_id=1, source_target_pairs={{0,64},{32,96},{64,0},{96,32},{1,65},{33,97},{65,1},{97,33},{2,66}... | collective-permute-start | bytes 786440 | tf_op jit(solution)/shard_map/ppermute | solution.py:263
  195.8 40.1 %collective-permute-start.10 = (f32[512,256]{1,0:T(8,128)}, f32[512,256]{1,0:T(8,128)S(1)}, u32[]{:S(2)}, u32[]{:S(2)}) collective-permute-start(f32[512,256]{1,0:T(8,128)} %copy-done.17), channel_id=1, source_target_pairs={{0,32},{32,0},{64,96},{96,64},{1,33},{33,1},{65,97},{97,65},{2,34}... | collective-permute-start | bytes 1572872 | tf_op jit(solution)/shard_map/ppermute | solution.py:263
  196.1 40.4 %collective-permute-start.11 = (f32[512,256]{1,0:T(8,128)}, f32[512,256]{1,0:T(8,128)S(1)}, u32[]{:S(2)}, u32[]{:S(2)}) collective-permute-start(f32[512,256]{1,0:T(8,128)} %copy-done.16), channel_id=1, source_target_pairs={{0,64},{32,96},{64,0},{96,32},{1,65},{33,97},{65,1},{97,33},{2,66}... | collective-permute-start | bytes 1572872 | tf_op jit(solution)/shard_map/ppermute | solution.py:263
  199.0 1.9 collective-permute-start.19
  200.9 2.8 collective-permute-start.25
  203.6 4.9 %collective-permute-start.24 = (f32[16,128]{1,0:T(8,128)S(1)}, f32[16,128]{1,0:T(8,128)S(1)}, u32[]{:S(2)}, u32[]{:S(2)}) collective-permute-start(f32[16,128]{1,0:T(8,128)S(1)} %add_add_fusion), channel_id=1, source_target_pairs={{0,6},{2,4},{4,2},{6,0},{1,7},{3,5},{5,3},{7,1},{8,14},{10,12},{12... | collective-permute-start | bytes 24584 | tf_op jit(solution)/shard_map/ppermute | solution.py:223
  208.6 4.0 %collective-permute-start.23 = (f32[16,128]{1,0:T(8,128)S(1)}, f32[16,128]{1,0:T(8,128)S(1)}, u32[]{:S(2)}, u32[]{:S(2)}) collective-permute-start(f32[16,128]{1,0:T(8,128)S(1)} %add_add_fusion), channel_id=1, source_target_pairs={{0,4},{2,6},{4,0},{6,2},{1,5},{3,7},{5,1},{7,3},{8,12},{10,14},{12... | collective-permute-start | bytes 24584 | tf_op jit(solution)/shard_map/ppermute | solution.py:223
  212.6 2.8 collective-permute-start.22
  215.4 20.5 %collective-permute-start.15 = (f32[512,128]{1,0:T(8,128)}, f32[512,128]{1,0:T(8,128)S(1)}, u32[]{:S(2)}, u32[]{:S(2)}) collective-permute-start(f32[512,128]{1,0:T(8,128)} %copy-done.18), channel_id=1, source_target_pairs={{0,96},{32,64},{64,32},{96,0},{1,97},{33,65},{65,33},{97,1},{2,98}... | collective-permute-start | bytes 786440 | tf_op jit(solution)/shard_map/ppermute | solution.py:263
  216.0 31.1 %collective-permute-start.12 = (f32[512,256]{1,0:T(8,128)}, f32[512,256]{1,0:T(8,128)S(1)}, u32[]{:S(2)}, u32[]{:S(2)}) collective-permute-start(f32[512,256]{1,0:T(8,128)} %copy-done.14), channel_id=1, source_target_pairs={{0,96},{32,64},{64,32},{96,0},{1,97},{33,65},{65,33},{97,1},{2,98}... | collective-permute-start | bytes 1572872 | tf_op jit(solution)/shard_map/ppermute | solution.py:263
  218.1 29.1 %collective-permute-start.7 = (f32[512,256]{1,0:T(8,128)}, f32[512,256]{1,0:T(8,128)S(1)}, u32[]{:S(2)}, u32[]{:S(2)}) collective-permute-start(f32[512,256]{1,0:T(8,128)} %copy-done.15), channel_id=1, source_target_pairs={{0,32},{32,0},{64,96},{96,64},{1,33},{33,1},{65,97},{97,65},{2,34}... | collective-permute-start | bytes 1572872 | tf_op jit(solution)/shard_map/ppermute | solution.py:263
  235.9 67.4 %collective-permute-start.4 = (f32[512,384]{1,0:T(8,128)}, f32[512,384]{1,0:T(8,128)S(1)}, u32[]{:S(2)}, u32[]{:S(2)}) collective-permute-start(f32[512,384]{1,0:T(8,128)} %copy-done.11), channel_id=1, source_target_pairs={{0,32},{32,0},{64,96},{96,64},{1,33},{33,1},{65,97},{97,65},{2,34}... | collective-permute-start | bytes 2359304 | tf_op jit(solution)/shard_map/ppermute | solution.py:263
  235.9 67.4 %collective-permute-start.5 = (f32[512,384]{1,0:T(8,128)}, f32[512,384]{1,0:T(8,128)S(1)}, u32[]{:S(2)}, u32[]{:S(2)}) collective-permute-start(f32[512,384]{1,0:T(8,128)} %copy-done.10), channel_id=1, source_target_pairs={{0,64},{32,96},{64,0},{96,32},{1,65},{33,97},{65,1},{97,33},{2,66}... | collective-permute-start | bytes 2359304 | tf_op jit(solution)/shard_map/ppermute | solution.py:263
  236.5 66.8 %collective-permute-start.6 = (f32[512,384]{1,0:T(8,128)}, f32[512,384]{1,0:T(8,128)S(1)}, u32[]{:S(2)}, u32[]{:S(2)}) collective-permute-start(f32[512,384]{1,0:T(8,128)} %copy-done.9), channel_id=1, source_target_pairs={{0,96},{32,64},{64,32},{96,0},{1,97},{33,65},{65,33},{97,1},{2,98}... | collective-permute-start | bytes 2359304 | tf_op jit(solution)/shard_map/ppermute | solution.py:263
  247.1 39.7 %collective-permute-start.8 = (f32[512,256]{1,0:T(8,128)}, f32[512,256]{1,0:T(8,128)S(1)}, u32[]{:S(2)}, u32[]{:S(2)}) collective-permute-start(f32[512,256]{1,0:T(8,128)} %copy-done.13), channel_id=1, source_target_pairs={{0,64},{32,96},{64,0},{96,32},{1,65},{33,97},{65,1},{97,33},{2,66}... | collective-permute-start | bytes 1572872 | tf_op jit(solution)/shard_map/ppermute | solution.py:263
  247.2 56.2 %collective-permute-start.9 = (f32[512,256]{1,0:T(8,128)}, f32[512,256]{1,0:T(8,128)S(1)}, u32[]{:S(2)}, u32[]{:S(2)}) collective-permute-start(f32[512,256]{1,0:T(8,128)} %copy-done.12), channel_id=1, source_target_pairs={{0,96},{32,64},{64,32},{96,0},{1,97},{33,65},{65,33},{97,1},{2,98}... | collective-permute-start | bytes 1572872 | tf_op jit(solution)/shard_map/ppermute | solution.py:263
  303.3 1.0 copy-start.5
